TPU v7x, 32 devices: a whole 2x2x4 slice. The times are simulated.
32 devices in a mesh: grp: 2 (over x), tp: 16 (over z, y, core).
Axes of the slice: x: 2, y: 2, z: 4, core: 2. Of those that a mesh axis runs over, the one named last changes fastest.
Arguments:
- hidden: bfloat16 [1024, 16384], P('grp', 'tp'), parts along dimension 0, may hold values from -36 to 36
- norm_gain: float32 [16384], P('tp'), may hold values from 0.3 to 10, as said below
- prefix: int32 [2], P('grp'), parts along dimension 0, may hold values from 0 to 8192
- w_query: bfloat16 [16384, 2048], P(None, 'tp'), may hold values from -0.046875 to 0.046875
- w_kv: bfloat16 [256, 16384], P('tp'), may hold values from -0.046875 to 0.046875
- w_scale: float32 [2304], P('tp'), may hold values from 0.25 to 4
Outputs:
- queries: bfloat16 [1024, 2048], P('grp', 'tp'), parts along dimension 0
- keys: bfloat16 [1024, 2048], P('grp', 'tp'), parts along dimension 0
- values: bfloat16 [1024, 2048], P('grp', 'tp'), parts along dimension 0
- payload: bfloat16 [1024, 16384], P('grp', 'tp'), parts along dimension 0
- row_scale: float32 [1024], P('grp'), parts along dimension 0
There are 2 independent parts, one for each index of `grp`. A program takes and returns all parts, laid end to end along the dimension named above; an argument that names none is the same for every part. Nothing has to cross between parts.
Inputs may be any that keep to these rules, and one draw needn't show every extreme that they name: `norm_gain`: positive.
All inputs are finite; a program needn't handle non-finite values. Where the computation divides by a largest or mean magnitude, that divisor is 1e-20 or more.
Results may differ from a plain program's by a relative error of at most 0.012.
Values may be sent and summed in bfloat16 or wider, within the bound.
A program may use at most 64 MiB of HBM per device.

v0:
```python
import functools

import jax
import jax.numpy as jnp
from jax import lax
from jax.experimental import pallas as pl
from jax.experimental.pallas import tpu as pltpu
from jax.sharding import PartitionSpec as P

HD = 128
KV_COLS_DEV = 8
norm_eps = 1e-05
tiny_eps = 1e-06
rope_base = 500000.0
PIECES = 2
GRID_PIECES = 4


def ring_order(chips):
    cols = 1
    while (2 * cols) * (2 * cols) <= chips and chips % (2 * cols) == 0:
        cols *= 2
    rows = chips // cols
    if cols < 2 or rows % 2:
        return list(range(chips))
    order = [0]
    for row in range(rows):
        span = range(1, cols) if row % 2 == 0 else range(cols - 1, 0, -1)
        order += [row * cols + col for col in span]
    order += [row * cols for row in range(rows - 1, 0, -1)]
    return order


def lookup(table, index):
    total = jnp.int32(0)
    for key, value in enumerate(table):
        total = total + jnp.where(index == key, jnp.int32(value), jnp.int32(0))
    return total


def spread(row):
    return jnp.transpose(jnp.broadcast_to(row, (128, 128)))


def kernel(
    n, width, prefix_ref, h_ref, gain_ref, freq_ref, qscale_ref, kvscale_ref, wq_hbm, wkv_hbm,
    q_out, k_out, v_out, payload_out, rs_out,
    gath, wq, wkv, acc, kvacc, part_q, part_kv, stat_own, stats, kv_own, kv_all, inv_col, cosine, sine,
    send_sem, recv_sem, st_send, st_recv, kv_send, kv_recv,
    wl_sem, wkl_sem, wr_send, wr_recv, wkr_send, wkr_recv, ex_send, ex_recv,
):
    me = lax.axis_index("tp")
    chips = n // 2
    core = lax.rem(me, 2)
    chip = me // 2
    mate = me + 1 - 2 * core
    count, depth = h_ref.shape
    half = count // 2
    rows = half // PIECES
    pieces = HD // KV_COLS_DEV
    kv_heads = n // pieces
    order = ring_order(chips)
    place = [order.index(c) for c in range(chips)]
    pos = lookup(place, chip)
    succ = 2 * lookup(order, lax.rem(pos + 1, chips)) + core
    pred = 2 * lookup(order, lax.rem(pos + chips - 1, chips)) + core

    barrier = pltpu.get_barrier_semaphore()

    def greet(d, carry):
        pl.semaphore_signal(barrier, inc=1, device_id={"tp": lax.rem(me + d, n)})
        return carry

    lax.fori_loop(1, n, greet, 0)

    own_wq = pltpu.make_async_copy(wq_hbm.at[:, core], wq.at[:, :, pl.ds(0, HD)], wl_sem)
    own_wq.start()

    def kv_local(k):
        cols = pl.ds(pl.multiple_of((2 * k + core) * depth, 128), depth)
        return pltpu.make_async_copy(wkv_hbm.at[:, cols], wkv.at[k, pl.ds(0, 16)], wkl_sem.at[k])

    def kv_remote(k):
        cols = pl.ds(pl.multiple_of((2 * k + 1 - core) * depth, 128), depth)
        return pltpu.make_async_remote_copy(
            wkv_hbm.at[:, cols], wkv.at[k, pl.ds(16, 16)], wkr_send.at[k], wkr_recv.at[k],
            device_id={"tp": mate},
        )

    mate_wq = pltpu.make_async_remote_copy(
        wq_hbm.at[:, 1 - core], wq.at[:, :, pl.ds(HD, HD)], wr_send, wr_recv, device_id={"tp": mate}
    )
    lax.fori_loop(0, chips, lambda k, c: (kv_local(k).start(), c)[1], 0)

    gain = gain_ref[...]
    for r in range(count // 128):
        block = pl.ds(r * 128, 128)
        wide = h_ref[block, :].astype(jnp.float32)
        weighted = wide * gain
        gath[0, block, :] = weighted.astype(jnp.bfloat16)
        square = jnp.sum(wide * wide, axis=1, keepdims=True)
        top = jnp.max(jnp.abs(weighted), axis=1, keepdims=True)
        stat_own[pl.ds(r, 1), :] = jnp.transpose(jnp.broadcast_to(square, (128, 128)))[0:1, :]
        stat_own[pl.ds(4 + r, 1), :] = jnp.transpose(jnp.broadcast_to(top, (128, 128)))[0:1, :]
    stats[me] = stat_own[...]

    pl.semaphore_wait(barrier, n - 1)

    def hop(step, way, piece):
        block = pl.ds(way * half + piece * rows, rows)
        return pltpu.make_async_remote_copy(
            gath.at[step, block], gath.at[step + 1, block],
            send_sem.at[step, way, piece], recv_sem.at[step, way, piece],
            device_id={"tp": succ if way == 0 else pred},
        )

    def multiply(step, way, piece):
        block = pl.ds(way * half + piece * rows, rows)
        shift = chips - step if way == 0 else step
        owner = lookup(order, lax.rem(pos + shift, chips))
        left = gath[step, block, :]
        acc[block, :] += jnp.dot(left, wq[owner], preferred_element_type=jnp.float32)
        kvacc[block, :] += lax.dot_general(
            left, wkv[owner], (((1,), (1,)), ((), ())), preferred_element_type=jnp.float32
        )

    for piece in range(PIECES):
        for way in range(2):
            hop(0, way, piece).start()
    mate_wq.start()
    lax.fori_loop(0, chips, lambda k, c: (kv_remote(k).start(), c)[1], 0)

    def stat_copy(d):
        return pltpu.make_async_remote_copy(
            stat_own, stats.at[me], st_send.at[d], st_recv.at[d], device_id={"tp": lax.rem(me + d, n)}
        )

    lax.fori_loop(1, n, lambda d, c: (stat_copy(d).start(), c)[1], 0)

    acc[...] = jnp.zeros_like(acc)
    kvacc[...] = jnp.zeros_like(kvacc)
    token = lax.broadcasted_iota(jnp.int32, (128, HD), 0) + prefix_ref[0]
    freq = freq_ref[...]
    even = lax.rem(lax.broadcasted_iota(jnp.int32, (128, HD), 1), 2) == 0
    for r in range(count // 128):
        angle = (token + r * 128).astype(jnp.float32) * freq
        cosine[pl.ds(r * 128, 128), :] = jnp.cos(angle)
        turn = jnp.sin(angle)
        sine[pl.ds(r * 128, 128), :] = jnp.where(even, -turn, turn)

    lax.fori_loop(1, n, lambda d, c: (stat_copy(d).wait(), c)[1], 0)
    everything = stats[...]
    inverse = 1.0 / jnp.sqrt(jnp.sum(everything[:, 0:4, :], axis=0) / width + norm_eps)
    row_scale = jnp.max(everything[:, 4:8, :], axis=0) * inverse + tiny_eps
    rs_out[...] = row_scale
    for r in range(count // 128):
        block = pl.ds(r * 128, 128)
        inv = spread(inverse[r : r + 1, :])
        inv_col[block, :] = inv
        scale = spread(row_scale[r : r + 1, :])
        for j in range(depth // 128):
            lanes = pl.ds(j * 128, 128)
            weighted = h_ref[block, lanes].astype(jnp.float32) * gain[:, j * 128 : j * 128 + 128]
            payload_out[block, lanes] = (weighted * inv / scale).astype(jnp.bfloat16)

    own_wq.wait()
    lax.fori_loop(0, chips, lambda k, c: (kv_local(k).wait(), c)[1], 0)
    mate_wq.wait()
    lax.fori_loop(0, chips, lambda k, c: (kv_remote(k).wait(), c)[1], 0)

    for piece in range(PIECES):
        for way in range(2):
            multiply(0, way, piece)

    def ring_step(step, carry):
        for piece in range(PIECES):
            for way in range(2):
                hop(step - 1, way, piece).wait_recv()
                hop(step, way, piece).start()
                multiply(step, way, piece)
        return carry

    lax.fori_loop(1, chips - 1, ring_step, 0)
    for piece in range(PIECES):
        for way in range(2):
            hop(chips - 2, way, piece).wait_recv()
            multiply(chips - 1, way, piece)

    ex_kv = pltpu.make_async_remote_copy(
        kvacc, part_kv, ex_send.at[0], ex_recv.at[0], device_id={"tp": mate}
    )
    ex_q = pltpu.make_async_remote_copy(
        acc.at[:, pl.ds(HD, HD)], part_q, ex_send.at[1], ex_recv.at[1], device_id={"tp": mate}
    )
    ex_kv.start()
    ex_q.start()

    def drain(step, carry):
        for piece in range(PIECES):
            for way in range(2):
                hop(step, way, piece).wait_send()
        return carry

    lax.fori_loop(0, chips - 1, drain, 0)
    ex_kv.wait()
    kvscale = kvscale_ref[...]
    for r in range(count // 128):
        block = pl.ds(r * 128, 128)
        cols = (kvacc[block, 0:16] + part_kv[block, 16:32]) * inv_col[block, 0:16] * kvscale
        cols = jnp.concatenate([cols, jnp.zeros((128, 112), jnp.float32)], axis=1)
        kv_own[:, block] = jnp.transpose(cols)[0:16, :].astype(jnp.bfloat16)

    my_head = me * kv_heads // n
    group = lax.rem(me, kv_heads)
    slot = me // kv_heads

    def kv_copy(i):
        return pltpu.make_async_remote_copy(
            kv_own, kv_all.at[slot], kv_send.at[i], kv_recv.at[slot],
            device_id={"tp": group * pieces + i},
        )

    def kv_arrival(i):
        return pltpu.make_async_remote_copy(
            kv_own, kv_all.at[i], kv_send.at[i], kv_recv.at[i], device_id={"tp": mate}
        )

    def kv_start(i, carry):
        @pl.when(group * pieces + i != me)
        def _():
            kv_copy(i).start()

        return carry

    def kv_wait(i, carry):
        @pl.when(group * pieces + i != me)
        def _():
            kv_copy(i).wait_send()

        @pl.when(i * kv_heads + my_head != me)
        def _():
            kv_arrival(i).wait_recv()

        return carry

    @pl.when(my_head == group)
    def _():
        kv_all[slot] = kv_own[...]

    lax.fori_loop(0, pieces, kv_start, 0)

    def rotated(x, block):
        swapped = jnp.where(even, pltpu.roll(x, HD - 1, 1), pltpu.roll(x, 1, 1))
        return (x * cosine[block, :] + swapped * sine[block, :]).astype(jnp.bfloat16)

    ex_q.wait()
    qscale = qscale_ref[...]
    for r in range(count // 128):
        block = pl.ds(r * 128, 128)
        x = (acc[block, 0:HD] + part_q[block, :]) * inv_col[block, :] * qscale
        q_out[block, :] = rotated(x, block)

    lax.fori_loop(0, pieces, kv_wait, 0)
    for r in range(count // 128):
        block = pl.ds(r * 128, 128)
        both = kv_all[:, :, block].astype(jnp.float32)
        keys = jnp.transpose(both[:, 0:KV_COLS_DEV, :].reshape(HD, 128))
        k_out[block, :] = rotated(keys, block)
        values = jnp.transpose(both[:, KV_COLS_DEV:, :].reshape(HD, 128))
        v_out[block, :] = values.astype(jnp.bfloat16)


def grid_kernel(
    width, prefix_ref, h_hbm, gain_hbm, freq_ref, scale_hbm, wq_hbm, wkv_hbm,
    q_out, k_out, v_out, payload_out, rs_out,
    gath, wq, wkv, wq2, wkv2, acc, kvacc, part_q, part_kv, far_q, far_kv, got_q, got_kv,
    stat_own, stats, kv_own, kv_all, inv_col, cosine, sine,
    send_sem, recv_sem, st_send, st_recv, kv_send, kv_recv,
    wl_sem, wkl_sem, wr_send, wr_recv, wkr_send, wkr_recv,
    wz_send, wz_recv, wx_send, wx_recv, ex_send, ex_recv,
    h_ref, gain_ref, scale_ref, in_sem,
):
    n = 16
    chips = 8
    me = lax.axis_index("tp")
    side = lax.axis_index("grp")
    core = lax.rem(me, 2)
    chip = me // 2
    y = lax.rem(chip, 2)
    z = chip // 2
    mate = me + 1 - 2 * core
    is_end = (z == 0) | (z == 3)
    is_mid = (z == 1) | (z == 2)
    inner = z + 1 - 2 * lax.rem(z, 2)
    neighbour = me + 4 * (inner - z)
    across = me + 4 * (3 - 2 * z)
    beside = me + 2 - 4 * y
    count, depth = h_ref.shape
    loads = [pltpu.make_async_copy(gain_hbm, gain_ref, in_sem.at[0])]
    for r in range(count // 128):
        block = pl.ds(r * 128, 128)
        loads.append(pltpu.make_async_copy(h_hbm.at[block], h_ref.at[block], in_sem.at[r + 1]))
    loads.append(pltpu.make_async_copy(scale_hbm, scale_ref, in_sem.at[count // 128 + 1]))
    for load in loads:
        load.start()
    rows = count // GRID_PIECES
    owners = [2 * z + y, 2 * (3 - z) + y, 2 * z + 1 - y, 2 * (3 - z) + 1 - y]
    theirs = [2 * inner + y, 2 * (3 - inner) + y, 2 * inner + 1 - y, 2 * (3 - inner) + 1 - y]

    barrier = pltpu.get_barrier_semaphore()

    def greet(d, carry):
        pl.semaphore_signal(barrier, inc=1, device_id={"tp": lax.rem(me + d, n)})
        return carry

    lax.fori_loop(1, n, greet, 0)
    pl.semaphore_signal(barrier, inc=1, device_id={"grp": 1 - side, "tp": me})

    own_wq = pltpu.make_async_copy(wq_hbm.at[:, core], wq.at[:, :, pl.ds(0, HD)], wl_sem)
    own_wq.start()

    def kv_local(k):
        cols = pl.ds(pl.multiple_of((2 * k + core) * depth, 128), depth)
        return pltpu.make_async_copy(wkv_hbm.at[:, cols], wkv.at[k, pl.ds(0, 16)], wkl_sem.at[k])

    def kv_remote(k):
        cols = pl.ds(pl.multiple_of((2 * k + 1 - core) * depth, 128), depth)
        return pltpu.make_async_remote_copy(
            wkv_hbm.at[:, cols], wkv.at[k, pl.ds(16, 16)], wkr_send.at[k], wkr_recv.at[k],
            device_id={"tp": mate},
        )

    mate_wq = pltpu.make_async_remote_copy(
        wq_hbm.at[:, 1 - core], wq.at[:, :, pl.ds(HD, HD)], wr_send, wr_recv, device_id={"tp": mate}
    )
    lax.fori_loop(0, chips, lambda k, c: (kv_local(k).start(), c)[1], 0)

    loads[0].wait()
    gain = gain_ref[...]
    for r in range(count // 128):
        block = pl.ds(r * 128, 128)
        loads[r + 1].wait()
        wide = h_ref[block, :].astype(jnp.float32)
        weighted = wide * gain
        gath[0, block, :] = weighted.astype(jnp.bfloat16)
        square = jnp.sum(wide * wide, axis=1, keepdims=True)
        top = jnp.max(jnp.abs(weighted), axis=1, keepdims=True)
        stat_own[pl.ds(r, 1), :] = jnp.transpose(jnp.broadcast_to(square, (128, 128)))[0:1, :]
        stat_own[pl.ds(4 + r, 1), :] = jnp.transpose(jnp.broadcast_to(top, (128, 128)))[0:1, :]
    stats[me] = stat_own[...]
    loads[-1].wait()

    pl.semaphore_wait(barrier, n)

    def move(kind, source, target, piece, device):
        block = pl.ds(piece * rows, rows)
        return pltpu.make_async_remote_copy(
            gath.at[source, block], gath.at[target, block],
            send_sem.at[kind, piece], recv_sem.at[target, piece], device_id={"tp": device},
        )

    def beside_own(p):
        return move(0, 0, 2, p, beside)

    def beside_far(p):
        return move(1, 1, 3, p, beside)

    def end_up(p):
        return move(2, 0, 4, p, neighbour)

    def mid_across(p):
        return move(2, 0, 1, p, across)

    def relay_across(p):
        return move(3, 4, 5, p, across)

    def relay_down(p):
        return move(4, 5, 1, p, neighbour)

    def part_of(ref, kv_ref, at, part):
        if part == 2:
            return kv_ref.at[at]
        return ref.at[at, :, pl.ds(part * HD, HD)]

    def weights_z(i, part):
        block = jnp.where(side == 0, theirs[2 * i], theirs[2 * i + 1])
        return pltpu.make_async_remote_copy(
            part_of(wq, wkv, block, part), part_of(wq2, wkv2, 2 * i + side, part),
            wz_send.at[i, part], wz_recv.at[i, part], device_id={"tp": neighbour},
        )

    def weights_x(i, part):
        piece = part_of(wq2, wkv2, 2 * i + side, part)
        return pltpu.make_async_remote_copy(
            piece, piece, wx_send.at[i, part], wx_recv.at[i, part],
            device_id={"grp": 1 - side, "tp": me},
        )

    def weights_pass(i, part):
        weights_z(i, part).wait_recv()
        weights_x(i, part).start()

    def stat_copy(d):
        return pltpu.make_async_remote_copy(
            stat_own, stats.at[me], st_send.at[d], st_recv.at[d], device_id={"tp": lax.rem(me + d, n)}
        )

    everyone = range(GRID_PIECES)
    early = GRID_PIECES // 2

    @pl.when(is_end)
    def _():
        for p in everyone:
            end_up(p).start()

    @pl.when(is_mid)
    def _():
        for p in everyone[:early]:
            mid_across(p).start()

    for p in everyone:
        beside_own(p).start()
    own_wq.wait()
    mate_wq.start()
    lax.fori_loop(0, chips, lambda k, c: (kv_remote(k).start(), c)[1], 0)
    for i in range(2):
        weights_z(i, 0).start()
    lax.fori_loop(1, n, lambda d, c: (stat_copy(d).start(), c)[1], 0)

    acc[...] = jnp.zeros_like(acc)
    kvacc[...] = jnp.zeros_like(kvacc)

    def product(slot, p, mine):
        block = pl.ds(p * rows, rows)
        left = gath[slot, block, :]
        right, right_kv = (wq[owners[slot]], wkv[owners[slot]]) if mine else (wq2[slot], wkv2[slot])
        lanes = pl.ds(0 if mine else 2 * HD, 2 * HD)
        kv_lanes = pl.ds(0 if mine else 32, 32)
        acc[block, lanes] += jnp.dot(left, right, preferred_element_type=jnp.float32)
        kvacc[block, kv_lanes] += lax.dot_general(
            left, right_kv, (((1,), (1,)), ((), ())), preferred_element_type=jnp.float32
        )

    def both(slot, p):
        product(slot, p, True)
        product(slot, p, False)

    def whole(slot, mine):
        for p in everyone:
            product(slot, p, mine)

    even = lax.rem(lax.broadcasted_iota(jnp.int32, (128, HD), 1), 2) == 0

    def tables():
        token = lax.broadcasted_iota(jnp.int32, (128, HD), 0) + prefix_ref[0]
        freq = freq_ref[...]
        for r in range(count // 128):
            angle = (token + r * 128).astype(jnp.float32) * freq
            cosine[pl.ds(r * 128, 128), :] = jnp.cos(angle)
            turn = jnp.sin(angle)
            sine[pl.ds(r * 128, 128), :] = jnp.where(even, -turn, turn)

    def row_statistics():
        lax.fori_loop(1, n, lambda d, c: (stat_copy(d).wait(), c)[1], 0)
        everything = stats[...]
        inverse = 1.0 / jnp.sqrt(jnp.sum(everything[:, 0:4, :], axis=0) / width + norm_eps)
        row_scale = jnp.max(everything[:, 4:8, :], axis=0) * inverse + tiny_eps
        rs_out[...] = row_scale
        for r in range(count // 128):
            block = pl.ds(r * 128, 128)
            inv = spread(inverse[r : r + 1, :])
            inv_col[block, :] = inv
            scale = spread(row_scale[r : r + 1, :])
            for j in range(depth // 128):
                lanes = pl.ds(j * 128, 128)
                weighted = h_ref[block, lanes].astype(jnp.float32) * gain_ref[:, lanes]
                payload_out[block, lanes] = (weighted * inv / scale).astype(jnp.bfloat16)

    def mate_weights():
        mate_wq.wait()
        lax.fori_loop(0, chips, lambda k, c: (kv_local(k).wait(), c)[1], 0)
        lax.fori_loop(0, chips, lambda k, c: (kv_remote(k).wait(), c)[1], 0)
        for i in range(2):
            weights_z(i, 1).start()
            weights_z(i, 2).start()

    def weights_settle():
        for i in range(2):
            for part in range(3):
                weights_x(i, part).wait()

    def own_beside():
        for p in everyone:
            beside_own(p).wait_recv()
        whole(2, True)

    @pl.when(is_mid)
    def _():
        mate_weights()
        for p in everyone[:early]:
            end_up(p).wait_recv()
            relay_across(p).start()
            mid_across(p).wait_recv()
            beside_far(p).start()
        tables()
        for p in everyone[early:]:
            end_up(p).wait_recv()
            relay_across(p).start()
            if p == GRID_PIECES - 1:
                for late in everyone[early:]:
                    mid_across(late).start()
            relay_across(p - early).wait_recv()
            relay_down(p - early).start()
        row_statistics()
        whole(0, True)
        for p in everyone[early:]:
            relay_across(p).wait_recv()
            relay_down(p).start()
        for i in range(2):
            weights_pass(i, 0)
        own_beside()
        for p in everyone[early:]:
            mid_across(p).wait_recv()
            beside_far(p).start()
        for i in range(2):
            weights_pass(i, 1)
            weights_pass(i, 2)
        whole(1, True)
        for p in everyone:
            beside_far(p).wait_recv()
            product(3, p, True)
        weights_settle()
        for slot in range(4):
            whole(slot, False)

    @pl.when(is_end)
    def _():
        mate_weights()
        tables()
        for i in range(2):
            weights_pass(i, 0)
        row_statistics()
        whole(0, True)
        weights_pass(0, 1)
        weights_pass(0, 2)
        own_beside()
        weights_pass(1, 1)
        weights_pass(1, 2)
        for p in everyone:
            relay_down(p).wait_recv()
            beside_far(p).start()
            product(1, p, True)
            if p == early:
                weights_settle()
                whole(0, False)
                whole(2, False)
        whole(1, False)
        for p in everyone:
            beside_far(p).wait_recv()
            both(3, p)

    def swap(source, target, i):
        return pltpu.make_async_remote_copy(
            source, target, ex_send.at[i], ex_recv.at[i], device_id={"tp": mate}
        )

    def hand(source, target, i):
        return pltpu.make_async_remote_copy(
            source, target, ex_send.at[i], ex_recv.at[i], device_id={"tp": neighbour}
        )

    swaps = [
        swap(acc.at[:, pl.ds(3 * HD, HD)], part_q.at[1], 0),
        swap(kvacc, part_kv, 1),
        swap(acc.at[:, pl.ds(HD, HD)], part_q.at[0], 2),
    ]
    hands = [hand(far_kv, got_kv, 3), hand(far_q, got_q, 4)]
    swaps[1].start()
    swaps[0].start()
    swaps[2].start()
    swaps[1].wait()
    pad = jnp.zeros((128, 112), jnp.float32)

    def kv_rows(block, low):
        cols = kvacc[block, low : low + 16] + part_kv[block, low + 16 : low + 32]
        return jnp.transpose(jnp.concatenate([cols, pad], axis=1))[0:16, :]

    for r in range(count // 128):
        block = pl.ds(r * 128, 128)
        far_kv[:, block] = kv_rows(block, 32)
    swaps[0].wait()
    for r in range(count // 128):
        block = pl.ds(r * 128, 128)
        far_q[block, :] = (acc[block, 2 * HD : 3 * HD] + part_q[1, block, :]).astype(jnp.bfloat16)
    hands[0].start()
    hands[1].start()

    for p in everyone:
        beside_own(p).wait_send()
        beside_far(p).wait_send()
    for i in range(2):
        for part in range(3):
            weights_z(i, part).wait_send()

    @pl.when(is_end)
    def _():
        for p in everyone:
            end_up(p).wait_send()

    @pl.when(is_mid)
    def _():
        for p in everyone:
            mid_across(p).wait_send()
            relay_across(p).wait_send()
            relay_down(p).wait_send()

    kv_scale = jnp.concatenate([scale_ref[:, HD:], jnp.zeros((1, 112), jnp.float32)], axis=1)
    kv_scale = spread(kv_scale)[0:16, :]
    hands[0].wait()
    for r in range(count // 128):
        block = pl.ds(r * 128, 128)
        inv = jnp.transpose(inv_col[block, :])[0:1, :]
        mine = (kv_rows(block, 0) + got_kv[:, block]) * inv * kv_scale
        kv_own[:, block] = mine.astype(jnp.bfloat16)
    kv_all[me] = kv_own[...]

    def kv_copy(d):
        return pltpu.make_async_remote_copy(
            kv_own, kv_all.at[me], kv_send.at[d], kv_recv.at[d], device_id={"tp": lax.rem(me + d, n)}
        )

    lax.fori_loop(1, n, lambda d, c: (kv_copy(d).start(), c)[1], 0)

    def rotated(x, block):
        swapped = jnp.where(even, pltpu.roll(x, HD - 1, 1), pltpu.roll(x, 1, 1))
        return (x * cosine[block, :] + swapped * sine[block, :]).astype(jnp.bfloat16)

    swaps[2].wait()
    hands[1].wait()
    qscale = scale_ref[:, 0:HD]
    for r in range(count // 128):
        block = pl.ds(r * 128, 128)
        x = acc[block, 0:HD] + part_q[0, block, :] + got_q[block, :].astype(jnp.float32)
        q_out[block, :] = rotated(x * inv_col[block, :] * qscale, block)

    lax.fori_loop(1, n, lambda d, c: (kv_copy(d).wait(), c)[1], 0)
    for r in range(count // 128):
        block = pl.ds(r * 128, 128)
        pair = kv_all[:, :, block].astype(jnp.float32)
        keys = jnp.transpose(pair[:, 0:KV_COLS_DEV, :].reshape(HD, 128))
        k_out[block, :] = rotated(keys, block)
        values = jnp.transpose(pair[:, KV_COLS_DEV:, :].reshape(HD, 128))
        v_out[block, :] = values.astype(jnp.bfloat16)


def grid_scratch(count, depth):
    dma = pltpu.SemaphoreType.DMA
    bf16, f32 = jnp.bfloat16, jnp.float32
    return [
        pltpu.VMEM((6, count, depth), bf16),
        pltpu.VMEM((8, depth, 2 * HD), bf16),
        pltpu.VMEM((8, 32, depth), bf16),
        pltpu.VMEM((4, depth, 2 * HD), bf16),
        pltpu.VMEM((4, 32, depth), bf16),
        pltpu.VMEM((count, 4 * HD), f32),
        pltpu.VMEM((count, 64), f32),
        pltpu.VMEM((2, count, HD), f32),
        pltpu.VMEM((count, 64), f32),
        pltpu.VMEM((count, HD), bf16),
        pltpu.VMEM((16, count), f32),
        pltpu.VMEM((count, HD), bf16),
        pltpu.VMEM((16, count), f32),
        pltpu.VMEM((8, 128), f32),
        pltpu.VMEM((16, 8, 128), f32),
        pltpu.VMEM((16, count), bf16),
        pltpu.VMEM((16, 16, count), bf16),
        pltpu.VMEM((count, HD), f32),
        pltpu.VMEM((count, HD), f32),
        pltpu.VMEM((count, HD), f32),
        dma((5, GRID_PIECES)),
        dma((6, GRID_PIECES)),
        dma((16,)),
        dma((16,)),
        dma((16,)),
        dma((16,)),
        dma,
        dma((8,)),
        dma,
        dma,
        dma((8,)),
        dma((8,)),
        dma((2, 3)),
        dma((2, 3)),
        dma((2, 3)),
        dma((2, 3)),
        dma((5,)),
        dma((5,)),
        pltpu.VMEM((count, depth), bf16),
        pltpu.VMEM((1, depth), f32),
        pltpu.VMEM((1, HD + 2 * KV_COLS_DEV), f32),
        dma((count // 128 + 2,)),
    ]


def local(n, groups, hidden, norm_gain, prefix, w_query, w_kv, w_scale):
    count, depth = hidden.shape
    chips = n // 2
    width = depth * n
    grid = n == 16 and groups == 2 and n * KV_COLS_DEV == HD
    columns = jnp.arange(HD, dtype=jnp.int32)
    pair_index = (columns // 2).astype(jnp.float32)
    freq = jnp.power(jnp.float32(rope_base), -(2.0 * pair_index) / HD)[None, :]
    pieces = HD // KV_COLS_DEV
    vmem = pl.BlockSpec(memory_space=pltpu.VMEM)
    hbm = pl.BlockSpec(memory_space=pltpu.HBM if grid else pl.ANY)
    dma = pltpu.SemaphoreType.DMA
    bf16, f32 = jnp.bfloat16, jnp.float32
    queries, keys, values, payload, row_scale = pl.pallas_call(
        functools.partial(grid_kernel, width) if grid else functools.partial(kernel, n, width),
        out_shape=(
            jax.ShapeDtypeStruct((count, HD), bf16),
            jax.ShapeDtypeStruct((count, HD), bf16),
            jax.ShapeDtypeStruct((count, HD), bf16),
            jax.ShapeDtypeStruct((count, depth), bf16),
            jax.ShapeDtypeStruct((count // 128, 128), f32),
        ),
        in_specs=[pl.BlockSpec(memory_space=pltpu.SMEM)]
        + ([hbm, hbm, vmem] + [hbm] * 3 if grid else [vmem] * 5 + [hbm] * 2),
        out_specs=(vmem,) * 5,
        scratch_shapes=grid_scratch(count, depth) if grid else [
            pltpu.VMEM((chips, count, depth), bf16),
            pltpu.VMEM((chips, depth, 2 * HD), bf16),
            pltpu.VMEM((chips, 32, depth), bf16),
            pltpu.VMEM((count, 2 * HD), f32),
            pltpu.VMEM((count, 32), f32),
            pltpu.VMEM((count, HD), f32),
            pltpu.VMEM((count, 32), f32),
            pltpu.VMEM((8, 128), f32),
            pltpu.VMEM((n, 8, 128), f32),
            pltpu.VMEM((2 * KV_COLS_DEV, count), bf16),
            pltpu.VMEM((pieces, 2 * KV_COLS_DEV, count), bf16),
            pltpu.VMEM((count, HD), f32),
            pltpu.VMEM((count, HD), f32),
            pltpu.VMEM((count, HD), f32),
            dma((chips, 2, PIECES)),
            dma((chips, 2, PIECES)),
            dma((n,)),
            dma((n,)),
            dma((pieces,)),
            dma((pieces,)),
            dma,
            dma((chips,)),
            dma,
            dma,
            dma((chips,)),
            dma((chips,)),
            dma((2,)),
            dma((2,)),
        ],
        compiler_params=pltpu.CompilerParams(
            collective_id=0, has_side_effects=True, vmem_limit_bytes=(63 if grid else 48) * 1024 * 1024
        ),
    )(
        prefix,
        hidden,
        norm_gain[None, :],
        freq,
        *([w_scale[None, :]] if grid else [w_scale[None, :HD], w_scale[None, HD:]]),
        w_query.reshape(chips, 2, depth, HD),
        w_kv,
    )
    return queries, keys, values, payload, row_scale.reshape(count)


def solution(mesh):
    return jax.shard_map(
        functools.partial(local, mesh.shape["tp"], mesh.shape["grp"]),
        mesh=mesh,
        in_specs=(P("grp", "tp"), P("tp"), P("grp"), P(None, "tp"), P("tp", None), P("tp")),
        out_specs=(P("grp", "tp"), P("grp", "tp"), P("grp", "tp"), P("grp", "tp"), P("grp")),
        check_vma=False,
    )
```

profile of v0, /device:TPU:0, one launch (start us, length us, event | category | flops | bytes accessed | tf_op | source)
XLA Modules:
  0.0 98.9 jit_solution(17815140975779697376)
XLA Ops:
  1.3 0.5 fusion.4.freq_ref
  1.8 88.9 %shard_map.101 = (bf16[512,128]{1,0:T(8,128)(2,1)}, bf16[512,128]{1,0:T(8,128)(2,1)}, bf16[512,128]{1,0:T(8,128)(2,1)}, bf16[512,1024]{1,0:T(8,128)(2,1)}, f32[4,128]{1,0:T(4,128)}) custom-call(s32[1]{0:T(128)S(6)} %copy.16.prefix_ref, bf16[512,1024]{1,0:T(8,128)(2,1)} %h_hbm.1, f32[1,1024]{1,0:T(1,128)} %bitcast.5, f32[1,128]{1,0:T(1,128)} %fusion.4.freq_ref, ...), custom_call_target="tpu_custom_call" | custom-call | tf_op jit(solution)/shard_map/pallas_call | solution.py:718
  90.7 1.6 %copy.17 = bf16[512,128]{1,0:T(8,128)(2,1)} copy(bf16[512,128]{1,0:T(8,128)(2,1)} %get-tuple-element.20) | data formatting | bytes 262144
  92.2 1.6 %copy.18 = bf16[512,128]{1,0:T(8,128)(2,1)} copy(bf16[512,128]{1,0:T(8,128)(2,1)} %get-tuple-element.21) | data formatting | bytes 262144
  93.8 1.6 %copy.19 = bf16[512,128]{1,0:T(8,128)(2,1)} copy(bf16[512,128]{1,0:T(8,128)(2,1)} %get-tuple-element.22) | data formatting | bytes 262144
  95.4 2.3 %copy.20 = bf16[512,1024]{1,0:T(8,128)(2,1)} copy(bf16[512,1024]{1,0:T(8,128)(2,1)} %get-tuple-element.23) | data formatting | bytes 2097152
  97.6 1.2 %copy.21 = f32[512]{0:T(512)} copy(f32[512]{0:T(512)} %bitcast.6) | data formatting | bytes 4096
where the time goes:
time: 99.1 us; the launch traced here: 98.9 us
  Pallas kernels  88.9 us (90%)
  local copies, waits for them, and re-layouts  8.21 us (8%)
  between operations  1.29 us (1%)
    pallas_call x1, Pallas kernels, local(): pl.pallas_call(functools.partial(grid_kernel, width) if grid else functoo...  88.9 us
    unnamed x5, local copies, waits for them, and re-layouts  8.21 us

commit v1 on v0

--- a/solution.py
+++ b/solution.py
@@ -2,6 +2,7 @@
 
 import jax
 import jax.numpy as jnp
+import numpy as np
 from jax import lax
 from jax.experimental import pallas as pl
 from jax.experimental.pallas import tpu as pltpu
@@ -702,14 +703,32 @@
     ]
 
 
+def finish_kernel(*refs):
+    sources, targets, sems = refs[0:5], refs[5:10], refs[10]
+    outs = [pltpu.make_async_copy(sources[i], targets[i], sems.at[i]) for i in range(5)]
+    for copy in outs:
+        copy.start()
+    for copy in outs:
+        copy.wait()
+
+
+def finish(*arrays):
+    return pl.pallas_call(
+        finish_kernel,
+        out_shape=tuple(jax.ShapeDtypeStruct(a.shape, a.dtype) for a in arrays),
+        in_specs=[pl.BlockSpec(memory_space=pltpu.VMEM)] * 5,
+        out_specs=(pl.BlockSpec(memory_space=pltpu.HBM),) * 5,
+        scratch_shapes=[pltpu.SemaphoreType.DMA((5,))], compiler_params=pltpu.CompilerParams(vmem_limit_bytes=2 * 1024 * 1024),
+    )(*arrays)
+
+
 def local(n, groups, hidden, norm_gain, prefix, w_query, w_kv, w_scale):
     count, depth = hidden.shape
     chips = n // 2
     width = depth * n
     grid = n == 16 and groups == 2 and n * KV_COLS_DEV == HD
-    columns = jnp.arange(HD, dtype=jnp.int32)
-    pair_index = (columns // 2).astype(jnp.float32)
-    freq = jnp.power(jnp.float32(rope_base), -(2.0 * pair_index) / HD)[None, :]
+    pair_index = np.arange(HD) // 2
+    freq = jnp.asarray(np.power(rope_base, -(2.0 * pair_index) / HD)[None, :], jnp.float32)
     pieces = HD // KV_COLS_DEV
     vmem = pl.BlockSpec(memory_space=pltpu.VMEM)
     hbm = pl.BlockSpec(memory_space=pltpu.HBM if grid else pl.ANY)
@@ -718,11 +737,11 @@
     queries, keys, values, payload, row_scale = pl.pallas_call(
         functools.partial(grid_kernel, width) if grid else functools.partial(kernel, n, width),
         out_shape=(
-            jax.ShapeDtypeStruct((count, HD), bf16),
-            jax.ShapeDtypeStruct((count, HD), bf16),
-            jax.ShapeDtypeStruct((count, HD), bf16),
-            jax.ShapeDtypeStruct((count, depth), bf16),
-            jax.ShapeDtypeStruct((count // 128, 128), f32),
+            pltpu.VMEM((count, HD), bf16),
+            pltpu.VMEM((count, HD), bf16),
+            pltpu.VMEM((count, HD), bf16),
+            pltpu.VMEM((count, depth), bf16),
+            pltpu.VMEM((count // 128, 128), f32),
         ),
         in_specs=[pl.BlockSpec(memory_space=pltpu.SMEM)]
         + ([hbm, hbm, vmem] + [hbm] * 3 if grid else [vmem] * 5 + [hbm] * 2),
@@ -758,7 +777,7 @@
             dma((2,)),
         ],
         compiler_params=pltpu.CompilerParams(
-            collective_id=0, has_side_effects=True, vmem_limit_bytes=(63 if grid else 48) * 1024 * 1024
+            collective_id=0, has_side_effects=True, vmem_limit_bytes=(58 if grid else 48) * 1024 * 1024
         ),
     )(
         prefix,
@@ -769,6 +788,7 @@
         w_query.reshape(chips, 2, depth, HD),
         w_kv,
     )
+    queries, keys, values, payload, row_scale = finish(queries, keys, values, payload, row_scale)
     return queries, keys, values, payload, row_scale.reshape(count)
 
 

time: 99.1 us -> 90.9 us (0.917)
  local copies, waits for them, and re-layouts: 8.21 us -> 0 us
    unnamed x5 -> x0, local copies, waits for them, and re-layouts: 8.21 us -> none
    pallas_call x0 -> x1, Pallas kernels: none -> 1.15 us  [finish(): pl.pallas_call(finish_kernel, out_shape=tuple((jax.ShapeDtypeStruct(a.sha...]
where the time goes in v1:
time: 90.9 us; the launch traced here: 90.7 us
  Pallas kernels  89.3 us (98%)
  between operations  1.45 us (2%)
    pallas_call x1, Pallas kernels, local(): pl.pallas_call(functools.partial(grid_kernel, width) if grid else functoo...  88.1 us

profile of v1, /device:TPU:0, one launch (start us, length us, event | category | flops | bytes accessed | tf_op | source)
XLA Modules:
  0.0 90.7 jit_solution(16505016802416553482)
XLA Ops:
  1.3 88.1 %shard_map.110 = (bf16[512,128]{1,0:T(8,128)(2,1)S(1)}, bf16[512,128]{1,0:T(8,128)(2,1)S(1)}, bf16[512,128]{1,0:T(8,128)(2,1)S(1)}, bf16[512,1024]{1,0:T(8,128)(2,1)S(1)}, f32[4,128]{1,0:T(4,128)S(1)}) custom-call(s32[1]{0:T(128)S(6)} %copy.12.prefix_ref, bf16[512,1024]{1,0:T(8,128)(2,1)} %h_hbm.1, f32[1,1024]{1,0:T(1,128)} %bitcast.5, ...), custom_call_target="tpu_custom_call" | custom-call | tf_op jit(solution)/shard_map/pallas_call | solution.py:737
  89.4 1.1 %shard_map.111 = (bf16[512,128]{1,0:T(8,128)(2,1)}, bf16[512,128]{1,0:T(8,128)(2,1)}, bf16[512,128]{1,0:T(8,128)(2,1)}, bf16[512,1024]{1,0:T(8,128)(2,1)}, f32[4,128]{1,0:T(4,128)}) custom-call(bf16[512,128]{1,0:T(8,128)(2,1)S(1)} %get-tuple-element.15.refs_0_, bf16[512,128]{1,0:T(8,128)(2,1)S(1)} %get-tuple-element.16.refs_1_, ...), custom_call_target="tpu_custom_call" | custom-call | tf_op jit(solution)/shard_map/pallas_call | solution.py:716

commit v2 on v1

--- a/solution.py
+++ b/solution.py
@@ -274,15 +274,13 @@
 def grid_kernel(
     width, prefix_ref, h_hbm, gain_hbm, freq_ref, scale_hbm, wq_hbm, wkv_hbm,
     q_out, k_out, v_out, payload_out, rs_out,
-    gath, wq, wkv, wq2, wkv2, acc, kvacc, part_q, part_kv, far_q, far_kv, got_q, got_kv,
-    stat_own, stats, kv_own, kv_all, inv_col, cosine, sine,
-    send_sem, recv_sem, st_send, st_recv, kv_send, kv_recv,
-    wl_sem, wkl_sem, wr_send, wr_recv, wkr_send, wkr_recv,
-    wz_send, wz_recv, wx_send, wx_recv, ex_send, ex_recv,
-    h_ref, gain_ref, scale_ref, in_sem,
+    gath, wq, wkv, acc, kvacc, q_give, q_got, kv_give, kv_got,
+    stat_own, stats, kv_own, kv_all, inv_row, inv_col, cosine, sine,
+    h_ref, gain_ref, scale_ref, in_sem, own_sem,
+    st_send, st_recv, w_send, w_recv, wx_send, wx_recv, act_send, act_recv, mate_send, mate_recv,
+    pq_send, pq_recv, pkv_send, pkv_recv, kv_send, kv_recv,
 ):
     n = 16
-    chips = 8
     me = lax.axis_index("tp")
     side = lax.axis_index("grp")
     core = lax.rem(me, 2)
@@ -293,10 +291,15 @@
     is_end = (z == 0) | (z == 3)
     is_mid = (z == 1) | (z == 2)
     inner = z + 1 - 2 * lax.rem(z, 2)
-    neighbour = me + 4 * (inner - z)
     across = me + 4 * (3 - 2 * z)
     beside = me + 2 - 4 * y
+    peers = [me, beside, me + 4 * (inner - z), beside + 4 * (inner - z)]
+    places = [(z, y), (z, 1 - y), (inner, y), (inner, 1 - y)]
     count, depth = h_ref.shape
+    kv_cols = 2 * KV_COLS_DEV
+    rows = count // GRID_PIECES
+    everyone = range(GRID_PIECES)
+
     loads = [pltpu.make_async_copy(gain_hbm, gain_ref, in_sem.at[0])]
     for r in range(count // 128):
         block = pl.ds(r * 128, 128)
@@ -304,9 +307,6 @@
     loads.append(pltpu.make_async_copy(scale_hbm, scale_ref, in_sem.at[count // 128 + 1]))
     for load in loads:
         load.start()
-    rows = count // GRID_PIECES
-    owners = [2 * z + y, 2 * (3 - z) + y, 2 * z + 1 - y, 2 * (3 - z) + 1 - y]
-    theirs = [2 * inner + y, 2 * (3 - inner) + y, 2 * inner + 1 - y, 2 * (3 - inner) + 1 - y]
 
     barrier = pltpu.get_barrier_semaphore()
 
@@ -317,24 +317,41 @@
     lax.fori_loop(1, n, greet, 0)
     pl.semaphore_signal(barrier, inc=1, device_id={"grp": 1 - side, "tp": me})
 
-    own_wq = pltpu.make_async_copy(wq_hbm.at[:, core], wq.at[:, :, pl.ds(0, HD)], wl_sem)
-    own_wq.start()
-
-    def kv_local(k):
-        cols = pl.ds(pl.multiple_of((2 * k + core) * depth, 128), depth)
-        return pltpu.make_async_copy(wkv_hbm.at[:, cols], wkv.at[k, pl.ds(0, 16)], wkl_sem.at[k])
-
-    def kv_remote(k):
-        cols = pl.ds(pl.multiple_of((2 * k + 1 - core) * depth, 128), depth)
-        return pltpu.make_async_remote_copy(
-            wkv_hbm.at[:, cols], wkv.at[k, pl.ds(16, 16)], wkr_send.at[k], wkr_recv.at[k],
-            device_id={"tp": mate},
-        )
-
-    mate_wq = pltpu.make_async_remote_copy(
-        wq_hbm.at[:, 1 - core], wq.at[:, :, pl.ds(HD, HD)], wr_send, wr_recv, device_id={"tp": mate}
-    )
-    lax.fori_loop(0, chips, lambda k, c: (kv_local(k).start(), c)[1], 0)
+    def weights(s, k, part):
+        zt, yt = places[s]
+        block = 2 * (2 * (zt + k * (3 - 2 * zt)) + yt) + part % 2
+        if part < 2:
+            return wq_hbm.at[block], wq.at[k, part, :, pl.ds(s * HD, HD)]
+        cols = pl.ds(pl.multiple_of(block * depth, 128), depth)
+        return wkv_hbm.at[:, cols], wkv.at[k, part - 2, pl.ds(s * kv_cols, kv_cols)]
+
+    def weights_own(k, part):
+        source, target = weights(0, k, part)
+        return pltpu.make_async_copy(source, target, own_sem.at[part // 2])
+
+    def weights_to(s, k, part):
+        source, target = weights(s, k, part)
+        return pltpu.make_async_remote_copy(
+            source, target, w_send.at[(s > 1) * 2 + part // 2],
+            w_recv.at[part // 2 if s == 1 else 4 * s - 6 + part], device_id={"tp": peers[s]},
+        )
+
+    def weights_all(send_sem, recv_sem, part):
+        whole = wq.at[:, :, :, pl.ds(0, HD)] if part < 2 else wkv.at[:, :, pl.ds(0, kv_cols)]
+        return pltpu.make_async_remote_copy(
+            whole, whole, send_sem, recv_sem, device_id={"tp": peers[1]}
+        )
+
+    def weights_twin(s, part):
+        piece = weights(s, side, part)[1]
+        return pltpu.make_async_remote_copy(
+            piece, piece, wx_send.at[part // 2], wx_recv.at[part // 2],
+            device_id={"grp": 1 - side, "tp": me},
+        )
+
+    for k in range(2):
+        for part in range(4):
+            weights_own(k, part).start()
 
     loads[0].wait()
     gain = gain_ref[...]
@@ -343,7 +360,7 @@
         loads[r + 1].wait()
         wide = h_ref[block, :].astype(jnp.float32)
         weighted = wide * gain
-        gath[0, block, :] = weighted.astype(jnp.bfloat16)
+        gath[core, block, :] = weighted.astype(jnp.bfloat16)
         square = jnp.sum(wide * wide, axis=1, keepdims=True)
         top = jnp.max(jnp.abs(weighted), axis=1, keepdims=True)
         stat_own[pl.ds(r, 1), :] = jnp.transpose(jnp.broadcast_to(square, (128, 128)))[0:1, :]
@@ -353,353 +370,260 @@
 
     pl.semaphore_wait(barrier, n)
 
-    def move(kind, source, target, piece, device):
-        block = pl.ds(piece * rows, rows)
-        return pltpu.make_async_remote_copy(
-            gath.at[source, block], gath.at[target, block],
-            send_sem.at[kind, piece], recv_sem.at[target, piece], device_id={"tp": device},
-        )
-
-    def beside_own(p):
-        return move(0, 0, 2, p, beside)
-
-    def beside_far(p):
-        return move(1, 1, 3, p, beside)
-
-    def end_up(p):
-        return move(2, 0, 4, p, neighbour)
-
-    def mid_across(p):
-        return move(2, 0, 1, p, across)
-
-    def relay_across(p):
-        return move(3, 4, 5, p, across)
-
-    def relay_down(p):
-        return move(4, 5, 1, p, neighbour)
-
-    def part_of(ref, kv_ref, at, part):
-        if part == 2:
-            return kv_ref.at[at]
-        return ref.at[at, :, pl.ds(part * HD, HD)]
-
-    def weights_z(i, part):
-        block = jnp.where(side == 0, theirs[2 * i], theirs[2 * i + 1])
-        return pltpu.make_async_remote_copy(
-            part_of(wq, wkv, block, part), part_of(wq2, wkv2, 2 * i + side, part),
-            wz_send.at[i, part], wz_recv.at[i, part], device_id={"tp": neighbour},
-        )
-
-    def weights_x(i, part):
-        piece = part_of(wq2, wkv2, 2 * i + side, part)
-        return pltpu.make_async_remote_copy(
-            piece, piece, wx_send.at[i, part], wx_recv.at[i, part],
-            device_id={"grp": 1 - side, "tp": me},
-        )
-
-    def weights_pass(i, part):
-        weights_z(i, part).wait_recv()
-        weights_x(i, part).start()
-
     def stat_copy(d):
         return pltpu.make_async_remote_copy(
-            stat_own, stats.at[me], st_send.at[d], st_recv.at[d], device_id={"tp": lax.rem(me + d, n)}
-        )
-
-    everyone = range(GRID_PIECES)
-    early = GRID_PIECES // 2
-
-    @pl.when(is_end)
-    def _():
-        for p in everyone:
-            end_up(p).start()
-
-    @pl.when(is_mid)
-    def _():
-        for p in everyone[:early]:
-            mid_across(p).start()
-
+            stat_own, stats.at[me], st_send, st_recv, device_id={"tp": lax.rem(me + d, n)}
+        )
+
+    def stat_all():
+        others = stats.at[pl.ds(1, n - 1)]
+        return pltpu.make_async_remote_copy(others, others, st_send, st_recv, device_id={"tp": mate})
+
+    def act_mate():
+        return pltpu.make_async_remote_copy(
+            gath.at[core], gath.at[core], mate_send, mate_recv.at[GRID_PIECES],
+            device_id={"tp": mate},
+        )
+
+    def act_across(p):
+        block = pl.ds(p * rows, rows)
+        return pltpu.make_async_remote_copy(
+            gath.at[core, block], gath.at[2 + core, block], act_send, act_recv.at[p],
+            device_id={"tp": across},
+        )
+
+    def act_pass(p):
+        block = pl.ds(p * rows, rows)
+        piece = gath.at[2 + core, block]
+        return pltpu.make_async_remote_copy(
+            piece, piece, mate_send, mate_recv.at[p], device_id={"tp": mate}
+        )
+
+    forwarded = [(s, part) for part in (2, 3, 0, 1) for s in (2, 3)]
+    lax.fori_loop(1, n, lambda d, c: (stat_copy(d).start(), c)[1], 0)
+    for s, part in forwarded:
+        weights_to(s, side, part).start()
     for p in everyone:
-        beside_own(p).start()
-    own_wq.wait()
-    mate_wq.start()
-    lax.fori_loop(0, chips, lambda k, c: (kv_remote(k).start(), c)[1], 0)
-    for i in range(2):
-        weights_z(i, 0).start()
-    lax.fori_loop(1, n, lambda d, c: (stat_copy(d).start(), c)[1], 0)
-
-    acc[...] = jnp.zeros_like(acc)
-    kvacc[...] = jnp.zeros_like(kvacc)
-
-    def product(slot, p, mine):
-        block = pl.ds(p * rows, rows)
-        left = gath[slot, block, :]
-        right, right_kv = (wq[owners[slot]], wkv[owners[slot]]) if mine else (wq2[slot], wkv2[slot])
-        lanes = pl.ds(0 if mine else 2 * HD, 2 * HD)
-        kv_lanes = pl.ds(0 if mine else 32, 32)
-        acc[block, lanes] += jnp.dot(left, right, preferred_element_type=jnp.float32)
-        kvacc[block, kv_lanes] += lax.dot_general(
-            left, right_kv, (((1,), (1,)), ((), ())), preferred_element_type=jnp.float32
-        )
-
-    def both(slot, p):
-        product(slot, p, True)
-        product(slot, p, False)
-
-    def whole(slot, mine):
-        for p in everyone:
-            product(slot, p, mine)
+        act_across(p).start()
+    act_mate().start()
+    for k in range(2):
+        for part in range(4):
+            weights_to(1, k, part).start()
 
     even = lax.rem(lax.broadcasted_iota(jnp.int32, (128, HD), 1), 2) == 0
-
-    def tables():
-        token = lax.broadcasted_iota(jnp.int32, (128, HD), 0) + prefix_ref[0]
-        freq = freq_ref[...]
-        for r in range(count // 128):
-            angle = (token + r * 128).astype(jnp.float32) * freq
-            cosine[pl.ds(r * 128, 128), :] = jnp.cos(angle)
-            turn = jnp.sin(angle)
-            sine[pl.ds(r * 128, 128), :] = jnp.where(even, -turn, turn)
-
-    def row_statistics():
-        lax.fori_loop(1, n, lambda d, c: (stat_copy(d).wait(), c)[1], 0)
-        everything = stats[...]
-        inverse = 1.0 / jnp.sqrt(jnp.sum(everything[:, 0:4, :], axis=0) / width + norm_eps)
-        row_scale = jnp.max(everything[:, 4:8, :], axis=0) * inverse + tiny_eps
-        rs_out[...] = row_scale
-        for r in range(count // 128):
-            block = pl.ds(r * 128, 128)
-            inv = spread(inverse[r : r + 1, :])
-            inv_col[block, :] = inv
-            scale = spread(row_scale[r : r + 1, :])
-            for j in range(depth // 128):
-                lanes = pl.ds(j * 128, 128)
-                weighted = h_ref[block, lanes].astype(jnp.float32) * gain_ref[:, lanes]
-                payload_out[block, lanes] = (weighted * inv / scale).astype(jnp.bfloat16)
-
-    def mate_weights():
-        mate_wq.wait()
-        lax.fori_loop(0, chips, lambda k, c: (kv_local(k).wait(), c)[1], 0)
-        lax.fori_loop(0, chips, lambda k, c: (kv_remote(k).wait(), c)[1], 0)
-        for i in range(2):
-            weights_z(i, 1).start()
-            weights_z(i, 2).start()
-
-    def weights_settle():
-        for i in range(2):
-            for part in range(3):
-                weights_x(i, part).wait()
-
-    def own_beside():
-        for p in everyone:
-            beside_own(p).wait_recv()
-        whole(2, True)
-
-    @pl.when(is_mid)
-    def _():
-        mate_weights()
-        for p in everyone[:early]:
-            end_up(p).wait_recv()
-            relay_across(p).start()
-            mid_across(p).wait_recv()
-            beside_far(p).start()
-        tables()
-        for p in everyone[early:]:
-            end_up(p).wait_recv()
-            relay_across(p).start()
-            if p == GRID_PIECES - 1:
-                for late in everyone[early:]:
-                    mid_across(late).start()
-            relay_across(p - early).wait_recv()
-            relay_down(p - early).start()
-        row_statistics()
-        whole(0, True)
-        for p in everyone[early:]:
-            relay_across(p).wait_recv()
-            relay_down(p).start()
-        for i in range(2):
-            weights_pass(i, 0)
-        own_beside()
-        for p in everyone[early:]:
-            mid_across(p).wait_recv()
-            beside_far(p).start()
-        for i in range(2):
-            weights_pass(i, 1)
-            weights_pass(i, 2)
-        whole(1, True)
-        for p in everyone:
-            beside_far(p).wait_recv()
-            product(3, p, True)
-        weights_settle()
-        for slot in range(4):
-            whole(slot, False)
-
-    @pl.when(is_end)
-    def _():
-        mate_weights()
-        tables()
-        for i in range(2):
-            weights_pass(i, 0)
-        row_statistics()
-        whole(0, True)
-        weights_pass(0, 1)
-        weights_pass(0, 2)
-        own_beside()
-        weights_pass(1, 1)
-        weights_pass(1, 2)
-        for p in everyone:
-            relay_down(p).wait_recv()
-            beside_far(p).start()
-            product(1, p, True)
-            if p == early:
-                weights_settle()
-                whole(0, False)
-                whole(2, False)
-        whole(1, False)
-        for p in everyone:
-            beside_far(p).wait_recv()
-            both(3, p)
-
-    def swap(source, target, i):
-        return pltpu.make_async_remote_copy(
-            source, target, ex_send.at[i], ex_recv.at[i], device_id={"tp": mate}
-        )
-
-    def hand(source, target, i):
-        return pltpu.make_async_remote_copy(
-            source, target, ex_send.at[i], ex_recv.at[i], device_id={"tp": neighbour}
-        )
-
-    swaps = [
-        swap(acc.at[:, pl.ds(3 * HD, HD)], part_q.at[1], 0),
-        swap(kvacc, part_kv, 1),
-        swap(acc.at[:, pl.ds(HD, HD)], part_q.at[0], 2),
-    ]
-    hands = [hand(far_kv, got_kv, 3), hand(far_q, got_q, 4)]
-    swaps[1].start()
-    swaps[0].start()
-    swaps[2].start()
-    swaps[1].wait()
-    pad = jnp.zeros((128, 112), jnp.float32)
-
-    def kv_rows(block, low):
-        cols = kvacc[block, low : low + 16] + part_kv[block, low + 16 : low + 32]
-        return jnp.transpose(jnp.concatenate([cols, pad], axis=1))[0:16, :]
-
+    token = lax.broadcasted_iota(jnp.int32, (128, HD), 0) + prefix_ref[0]
+    freq = freq_ref[...]
+    for r in range(count // 128):
+        angle = (token + r * 128).astype(jnp.float32) * freq
+        cosine[pl.ds(r * 128, 128), :] = jnp.cos(angle)
+        turn = jnp.sin(angle)
+        sine[pl.ds(r * 128, 128), :] = jnp.where(even, -turn, turn)
+
+    stat_all().wait()
+    everything = stats[...]
+    inverse = 1.0 / jnp.sqrt(jnp.sum(everything[:, 0:4, :], axis=0) / width + norm_eps)
+    row_scale = jnp.max(everything[:, 4:8, :], axis=0) * inverse + tiny_eps
+    rs_out[...] = row_scale
+    inv_row[...] = inverse
     for r in range(count // 128):
         block = pl.ds(r * 128, 128)
-        far_kv[:, block] = kv_rows(block, 32)
-    swaps[0].wait()
-    for r in range(count // 128):
-        block = pl.ds(r * 128, 128)
-        far_q[block, :] = (acc[block, 2 * HD : 3 * HD] + part_q[1, block, :]).astype(jnp.bfloat16)
-    hands[0].start()
-    hands[1].start()
-
-    for p in everyone:
-        beside_own(p).wait_send()
-        beside_far(p).wait_send()
-    for i in range(2):
-        for part in range(3):
-            weights_z(i, part).wait_send()
-
-    @pl.when(is_end)
-    def _():
-        for p in everyone:
-            end_up(p).wait_send()
+        inv = spread(inverse[r : r + 1, :])
+        inv_col[block, :] = inv
+        scale = spread(row_scale[r : r + 1, :])
+        for j in range(depth // 128):
+            lanes = pl.ds(j * 128, 128)
+            weighted = h_ref[block, lanes].astype(jnp.float32) * gain_ref[:, lanes]
+            payload_out[block, lanes] = (weighted * inv / scale).astype(jnp.bfloat16)
+
+    for s, part in forwarded:
+        weights_to(s, side, part).wait_recv()
+        weights_twin(s, part).start()
 
     @pl.when(is_mid)
     def _():
         for p in everyone:
-            mid_across(p).wait_send()
-            relay_across(p).wait_send()
-            relay_down(p).wait_send()
-
-    kv_scale = jnp.concatenate([scale_ref[:, HD:], jnp.zeros((1, 112), jnp.float32)], axis=1)
-    kv_scale = spread(kv_scale)[0:16, :]
-    hands[0].wait()
-    for r in range(count // 128):
-        block = pl.ds(r * 128, 128)
-        inv = jnp.transpose(inv_col[block, :])[0:1, :]
-        mine = (kv_rows(block, 0) + got_kv[:, block]) * inv * kv_scale
-        kv_own[:, block] = mine.astype(jnp.bfloat16)
-    kv_all[me] = kv_own[...]
-
-    def kv_copy(d):
-        return pltpu.make_async_remote_copy(
-            kv_own, kv_all.at[me], kv_send.at[d], kv_recv.at[d], device_id={"tp": lax.rem(me + d, n)}
-        )
-
-    lax.fori_loop(1, n, lambda d, c: (kv_copy(d).start(), c)[1], 0)
+            act_across(p).wait_recv()
+            act_pass(p).start()
+
+    act_mate().wait_recv()
+    for part in (0, 2):
+        whole = weights_all(own_sem.at[part // 2], own_sem.at[part // 2], part)
+        whole.wait_recv()
+        weights_all(w_send.at[part // 2], w_recv.at[part // 2], part).wait()
+        weights_all(wx_send.at[part // 2], wx_recv.at[part // 2], part).wait()
+
+    def product(slot, block, k, half):
+        return jnp.dot(gath[slot, block, :], wq[k, half], preferred_element_type=jnp.float32)
+
+    def kv_product(slot, block, k, half):
+        return lax.dot_general(
+            wkv[k, half], gath[slot, block, :], (((1,), (1,)), ((), ())), preferred_element_type=jnp.float32
+        )
+
+    for p in everyone:
+        block = pl.ds(p * rows, rows)
+        kvacc[p] = kv_product(0, block, 0, 0) + kv_product(1, block, 0, 1)
+        acc[block, :] = product(0, block, 0, 0) + product(1, block, 0, 1)
+
+    def q_partial(s, p):
+        block = pl.ds(p * rows, rows)
+        return pltpu.make_async_remote_copy(
+            q_give.at[s - 1, block], q_got.at[s - 1, block], pq_send, pq_recv.at[p],
+            device_id={"tp": peers[s]},
+        )
+
+    def kv_partial(s, p):
+        return pltpu.make_async_remote_copy(
+            kv_give.at[s - 1, p], kv_got.at[s - 1, p], pkv_send, pkv_recv.at[p],
+            device_id={"tp": peers[s]},
+        )
+
+    def near(p):
+        block = pl.ds(p * rows, rows)
+        kvacc[p] += kv_product(2 + core, block, 1, core)
+        acc[block, :] += product(2 + core, block, 1, core)
+
+    def far(p):
+        block = pl.ds(p * rows, rows)
+        act_pass(p).wait_recv()
+        pair = kvacc[p] + kv_product(3 - core, block, 1, 1 - core)
+        kvacc[p] = pair
+        for s in range(1, 4):
+            kv_give[s - 1, p] = pair[s * kv_cols : (s + 1) * kv_cols, :]
+        for s in range(1, 4):
+            kv_partial(s, p).start()
+        whole = acc[block, :] + product(3 - core, block, 1, 1 - core)
+        acc[block, 0:HD] = whole[:, 0:HD]
+        for s in range(1, 4):
+            q_give[s - 1, block, :] = whole[:, s * HD : (s + 1) * HD].astype(jnp.bfloat16)
+        for s in range(1, 4):
+            q_partial(s, p).start()
+
+    kv_scale = jnp.concatenate([scale_ref[:, HD:], jnp.zeros((1, 128 - kv_cols), jnp.float32)], axis=1)
+    kv_scale = spread(kv_scale)[0:kv_cols, :]
+    qscale = scale_ref[:, 0:HD]
+
+    def kv_copy(p, d):
+        return pltpu.make_async_remote_copy(
+            kv_own.at[p], kv_all.at[me, p], kv_send, kv_recv.at[p], device_id={"tp": lax.rem(me + d, n)}
+        )
+
+    def every(ref, send_sem, recv_sem):
+        return pltpu.make_async_remote_copy(ref, ref, send_sem, recv_sem, device_id={"tp": mate})
+
+    def kv_reduce(p):
+        total = kvacc[p, 0:kv_cols, :]
+        every(kv_got.at[:, p], pkv_send, pkv_recv.at[p]).wait_recv()
+        for s in range(1, 4):
+            total = total + kv_got[s - 1, p]
+        mine = (total * inv_row[p : p + 1, :] * kv_scale).astype(jnp.bfloat16)
+        kv_own[p] = mine
+        kv_all[me, p] = mine
+        lax.fori_loop(1, n, lambda d, c: (kv_copy(p, d).start(), c)[1], 0)
 
     def rotated(x, block):
         swapped = jnp.where(even, pltpu.roll(x, HD - 1, 1), pltpu.roll(x, 1, 1))
         return (x * cosine[block, :] + swapped * sine[block, :]).astype(jnp.bfloat16)
 
-    swaps[2].wait()
-    hands[1].wait()
-    qscale = scale_ref[:, 0:HD]
-    for r in range(count // 128):
-        block = pl.ds(r * 128, 128)
-        x = acc[block, 0:HD] + part_q[0, block, :] + got_q[block, :].astype(jnp.float32)
+    def q_reduce(p):
+        block = pl.ds(p * rows, rows)
+        x = acc[block, 0:HD]
+        every(q_got.at[:, block], pq_send, pq_recv.at[p]).wait_recv()
+        for s in range(1, 4):
+            x = x + q_got[s - 1, block, :].astype(jnp.float32)
         q_out[block, :] = rotated(x * inv_col[block, :] * qscale, block)
 
-    lax.fori_loop(1, n, lambda d, c: (kv_copy(d).wait(), c)[1], 0)
-    for r in range(count // 128):
-        block = pl.ds(r * 128, 128)
-        pair = kv_all[:, :, block].astype(jnp.float32)
+    def heads(p):
+        block = pl.ds(p * rows, rows)
+        every(kv_all.at[pl.ds(1, n - 1), p], kv_send, kv_recv.at[p]).wait_recv()
+        pair = kv_all[:, p].astype(jnp.float32)
         keys = jnp.transpose(pair[:, 0:KV_COLS_DEV, :].reshape(HD, 128))
         k_out[block, :] = rotated(keys, block)
         values = jnp.transpose(pair[:, KV_COLS_DEV:, :].reshape(HD, 128))
         v_out[block, :] = values.astype(jnp.bfloat16)
 
+    last = GRID_PIECES - 1
+
+    @pl.when(is_mid)
+    def _():
+        for p in everyone:
+            near(p)
+        for p in everyone:
+            far(p)
+        for p in range(last):
+            kv_reduce(p)
+
+    @pl.when(is_end)
+    def _():
+        for p in everyone:
+            act_across(p).wait_recv()
+            act_pass(p).start()
+            near(p)
+            far(p)
+            if p:
+                kv_reduce(p - 1)
+
+    every(gath.at[0], act_send, act_send).wait_send()
+    every(gath.at[pl.ds(0, 2)], mate_send, mate_send).wait_send()
+    for part in (0, 2):
+        weights_all(w_send.at[2 + part // 2], w_send.at[2 + part // 2], part).wait_send()
+
+    for p in range(last):
+        q_reduce(p)
+    kv_reduce(last)
+    for p in range(last):
+        heads(p)
+    q_reduce(last)
+    every(kv_give, pkv_send, pkv_send).wait_send()
+    every(q_give, pq_send, pq_send).wait_send()
+    every(kv_all.at[pl.ds(1, n - 1)], kv_send, kv_send).wait_send()
+    heads(last)
+
 
 def grid_scratch(count, depth):
     dma = pltpu.SemaphoreType.DMA
     bf16, f32 = jnp.bfloat16, jnp.float32
+    pieces, kv_cols = GRID_PIECES, 2 * KV_COLS_DEV
+    rows = count // pieces
     return [
-        pltpu.VMEM((6, count, depth), bf16),
-        pltpu.VMEM((8, depth, 2 * HD), bf16),
-        pltpu.VMEM((8, 32, depth), bf16),
-        pltpu.VMEM((4, depth, 2 * HD), bf16),
-        pltpu.VMEM((4, 32, depth), bf16),
+        pltpu.VMEM((4, count, depth), bf16),
+        pltpu.VMEM((2, 2, depth, 4 * HD), bf16),
+        pltpu.VMEM((2, 2, 4 * kv_cols, depth), bf16),
         pltpu.VMEM((count, 4 * HD), f32),
-        pltpu.VMEM((count, 64), f32),
-        pltpu.VMEM((2, count, HD), f32),
-        pltpu.VMEM((count, 64), f32),
-        pltpu.VMEM((count, HD), bf16),
-        pltpu.VMEM((16, count), f32),
-        pltpu.VMEM((count, HD), bf16),
-        pltpu.VMEM((16, count), f32),
+        pltpu.VMEM((pieces, 4 * kv_cols, rows), f32),
+        pltpu.VMEM((3, count, HD), bf16),
+        pltpu.VMEM((3, count, HD), bf16),
+        pltpu.VMEM((3, pieces, kv_cols, rows), f32),
+        pltpu.VMEM((3, pieces, kv_cols, rows), f32),
         pltpu.VMEM((8, 128), f32),
         pltpu.VMEM((16, 8, 128), f32),
-        pltpu.VMEM((16, count), bf16),
-        pltpu.VMEM((16, 16, count), bf16),
+        pltpu.VMEM((pieces, kv_cols, rows), bf16),
+        pltpu.VMEM((16, pieces, kv_cols, rows), bf16),
+        pltpu.VMEM((count // 128, 128), f32),
         pltpu.VMEM((count, HD), f32),
         pltpu.VMEM((count, HD), f32),
         pltpu.VMEM((count, HD), f32),
-        dma((5, GRID_PIECES)),
-        dma((6, GRID_PIECES)),
-        dma((16,)),
-        dma((16,)),
-        dma((16,)),
-        dma((16,)),
-        dma,
-        dma((8,)),
+        pltpu.VMEM((count, depth), bf16),
+        pltpu.VMEM((1, depth), f32),
+        pltpu.VMEM((1, HD + kv_cols), f32),
+        dma((count // 128 + 2,)),
+        dma((2,)),
         dma,
         dma,
-        dma((8,)),
-        dma((8,)),
-        dma((2, 3)),
-        dma((2, 3)),
-        dma((2, 3)),
-        dma((2, 3)),
-        dma((5,)),
-        dma((5,)),
-        pltpu.VMEM((count, depth), bf16),
-        pltpu.VMEM((1, depth), f32),
-        pltpu.VMEM((1, HD + 2 * KV_COLS_DEV), f32),
-        dma((count // 128 + 2,)),
+        dma((4,)),
+        dma((10,)),
+        dma((2,)),
+        dma((2,)),
+        dma,
+        dma((pieces,)),
+        dma,
+        dma((pieces + 1,)),
+        dma,
+        dma((pieces,)),
+        dma,
+        dma((pieces,)),
+        dma,
+        dma((pieces,)),
     ]
 
 
@@ -726,7 +650,7 @@
     count, depth = hidden.shape
     chips = n // 2
     width = depth * n
-    grid = n == 16 and groups == 2 and n * KV_COLS_DEV == HD
+    grid = n == 16 and groups == 2 and n * KV_COLS_DEV == HD and count == 128 * GRID_PIECES
     pair_index = np.arange(HD) // 2
     freq = jnp.asarray(np.power(rope_base, -(2.0 * pair_index) / HD)[None, :], jnp.float32)
     pieces = HD // KV_COLS_DEV
@@ -777,7 +701,7 @@
             dma((2,)),
         ],
         compiler_params=pltpu.CompilerParams(
-            collective_id=0, has_side_effects=True, vmem_limit_bytes=(58 if grid else 48) * 1024 * 1024
+            collective_id=0, has_side_effects=True, vmem_limit_bytes=(60 if grid else 48) * 1024 * 1024
         ),
     )(
         prefix,
@@ -785,7 +709,7 @@
         norm_gain[None, :],
         freq,
         *([w_scale[None, :]] if grid else [w_scale[None, :HD], w_scale[None, HD:]]),
-        w_query.reshape(chips, 2, depth, HD),
+        w_query.reshape(n, depth, HD) if grid else w_query.reshape(chips, 2, depth, HD),
         w_kv,
     )
     queries, keys, values, payload, row_scale = finish(queries, keys, values, payload, row_scale)

time: 90.9 us -> 73.3 us (0.81)
  Pallas kernels: 89.3 us -> 71.8 us
    pallas_call x1, Pallas kernels: 88.1 us -> 70.7 us  [local(): pl.pallas_call(functools.partial(grid_kernel, width) if grid else functoo...]
where the time goes in v2:
time: 73.3 us; the launch traced here: 73.1 us
  Pallas kernels  71.8 us (98%)
  between operations  1.29 us (2%)
    pallas_call x1, Pallas kernels, local(): pl.pallas_call(functools.partial(grid_kernel, width) if grid else functoo...  70.7 us

profile of v2, /device:TPU:0, one launch (start us, length us, event | category | flops | bytes accessed | tf_op | source)
XLA Modules:
  0.0 73.1 jit_solution(11275619520689532137)
XLA Ops:
  1.3 70.7 %shard_map.110 = (bf16[512,128]{1,0:T(8,128)(2,1)S(1)}, bf16[512,128]{1,0:T(8,128)(2,1)S(1)}, bf16[512,128]{1,0:T(8,128)(2,1)S(1)}, bf16[512,1024]{1,0:T(8,128)(2,1)S(1)}, f32[4,128]{1,0:T(4,128)S(1)}) custom-call(s32[1]{0:T(128)S(6)} %copy.12.prefix_ref, bf16[512,1024]{1,0:T(8,128)(2,1)} %h_hbm.1, f32[1,1024]{1,0:T(1,128)} %bitcast.5, ...), custom_call_target="tpu_custom_call" | custom-call | tf_op jit(solution)/shard_map/pallas_call | solution.py:661
  72.0 1.1 %shard_map.111 = (bf16[512,128]{1,0:T(8,128)(2,1)}, bf16[512,128]{1,0:T(8,128)(2,1)}, bf16[512,128]{1,0:T(8,128)(2,1)}, bf16[512,1024]{1,0:T(8,128)(2,1)}, f32[4,128]{1,0:T(4,128)}) custom-call(bf16[512,128]{1,0:T(8,128)(2,1)S(1)} %get-tuple-element.15.refs_0_, bf16[512,128]{1,0:T(8,128)(2,1)S(1)} %get-tuple-element.16.refs_1_, ...), custom_call_target="tpu_custom_call" | custom-call | tf_op jit(solution)/shard_map/pallas_call | solution.py:640

commit v3 on v2

--- a/solution.py
+++ b/solution.py
@@ -15,6 +15,7 @@
 rope_base = 500000.0
 PIECES = 2
 GRID_PIECES = 4
+LATE = 384
 
 
 def ring_order(chips):
@@ -272,12 +273,12 @@
 
 
 def grid_kernel(
-    width, prefix_ref, h_hbm, gain_hbm, freq_ref, scale_hbm, wq_hbm, wkv_hbm,
+    width, prefix_ref, h_hbm, gain_hbm, freq_hbm, scale_hbm, wq_hbm, wkv_hbm,
     q_out, k_out, v_out, payload_out, rs_out,
-    gath, wq, wkv, acc, kvacc, q_give, q_got, kv_give, kv_got,
-    stat_own, stats, kv_own, kv_all, inv_row, inv_col, cosine, sine,
-    h_ref, gain_ref, scale_ref, in_sem, own_sem,
-    st_send, st_recv, w_send, w_recv, wx_send, wx_recv, act_send, act_recv, mate_send, mate_recv,
+    gath, wq, wkv, wq_late, acc, kvacc, q_give, q_got, kv_give, kv_got,
+    stat_own, stat_mate, stats, kv_own, kv_all, kv_tail, inv_row, inv_col, cosine, sine,
+    h_ref, gain_ref, scale_ref, freq_ref, in_sem, own_sem, late_send, late_recv,
+    st_send, st_recv, w_send, w_recv, wx_recv, wy_recv, act_send, act_recv, mate_send, mate_recv,
     pq_send, pq_recv, pkv_send, pkv_recv, kv_send, kv_recv,
 ):
     n = 16
@@ -299,60 +300,83 @@
     kv_cols = 2 * KV_COLS_DEV
     rows = count // GRID_PIECES
     everyone = range(GRID_PIECES)
+    last = GRID_PIECES - 1
+
+    barrier = pltpu.get_barrier_semaphore()
+
+    def greet(d, carry):
+        pl.semaphore_signal(barrier, inc=1, device_id={"tp": lax.rem(me + d, n)})
+        return carry
+
+    lax.fori_loop(1, n, greet, 0)
+    pl.semaphore_signal(barrier, inc=1, device_id={"grp": 1 - side, "tp": me})
 
     loads = [pltpu.make_async_copy(gain_hbm, gain_ref, in_sem.at[0])]
     for r in range(count // 128):
         block = pl.ds(r * 128, 128)
         loads.append(pltpu.make_async_copy(h_hbm.at[block], h_ref.at[block], in_sem.at[r + 1]))
     loads.append(pltpu.make_async_copy(scale_hbm, scale_ref, in_sem.at[count // 128 + 1]))
+    loads.append(pltpu.make_async_copy(freq_hbm, freq_ref, in_sem.at[count // 128 + 2]))
     for load in loads:
         load.start()
 
-    barrier = pltpu.get_barrier_semaphore()
-
-    def greet(d, carry):
-        pl.semaphore_signal(barrier, inc=1, device_id={"tp": lax.rem(me + d, n)})
-        return carry
-
-    lax.fori_loop(1, n, greet, 0)
-    pl.semaphore_signal(barrier, inc=1, device_id={"grp": 1 - side, "tp": me})
-
-    def weights(s, k, part):
+    def weights(s, k, half, kv):
         zt, yt = places[s]
-        block = 2 * (2 * (zt + k * (3 - 2 * zt)) + yt) + part % 2
-        if part < 2:
-            return wq_hbm.at[block], wq.at[k, part, :, pl.ds(s * HD, HD)]
+        block = 2 * (2 * (zt + k * (3 - 2 * zt)) + yt) + half
+        if not kv:
+            first = pl.ds(0, depth - LATE if s == 2 and k else depth)
+            return wq_hbm.at[block, first], wq.at[k, half, first, pl.ds(s * HD, HD)]
         cols = pl.ds(pl.multiple_of(block * depth, 128), depth)
-        return wkv_hbm.at[:, cols], wkv.at[k, part - 2, pl.ds(s * kv_cols, kv_cols)]
-
-    def weights_own(k, part):
-        source, target = weights(0, k, part)
-        return pltpu.make_async_copy(source, target, own_sem.at[part // 2])
-
-    def weights_to(s, k, part):
-        source, target = weights(s, k, part)
-        return pltpu.make_async_remote_copy(
-            source, target, w_send.at[(s > 1) * 2 + part // 2],
-            w_recv.at[part // 2 if s == 1 else 4 * s - 6 + part], device_id={"tp": peers[s]},
-        )
-
-    def weights_all(send_sem, recv_sem, part):
-        whole = wq.at[:, :, :, pl.ds(0, HD)] if part < 2 else wkv.at[:, :, pl.ds(0, kv_cols)]
-        return pltpu.make_async_remote_copy(
-            whole, whole, send_sem, recv_sem, device_id={"tp": peers[1]}
-        )
-
-    def weights_twin(s, part):
-        piece = weights(s, side, part)[1]
-        return pltpu.make_async_remote_copy(
-            piece, piece, wx_send.at[part // 2], wx_recv.at[part // 2],
-            device_id={"grp": 1 - side, "tp": me},
-        )
+        return wkv_hbm.at[:, cols], wkv.at[k, half, pl.ds(s * kv_cols, kv_cols)]
+
+    def weights_own(k, half, kv):
+        source, target = weights(0, k, half, kv)
+        return pltpu.make_async_copy(source, target, own_sem.at[k, kv])
+
+    def weights_beside(k, half, kv):
+        source, target = weights(1, k, half, kv)
+        return pltpu.make_async_remote_copy(
+            source, target, w_send.at[kv], wy_recv.at[k, kv], device_id={"tp": beside}
+        )
+
+    def weights_far(s, k, kv):
+        source, target = weights(s, k, side, kv)
+        return pltpu.make_async_remote_copy(
+            source, target, w_send.at[4 if kv else 2 + k], w_recv.at[s - 2, k, kv], device_id={"tp": peers[s]}
+        )
+
+    def weights_twin(s, k, kv):
+        piece = weights(s, k, side, kv)[1]
+        return pltpu.make_async_remote_copy(
+            piece, piece, w_send.at[7 if kv else 5 + k], wx_recv.at[k, kv], device_id={"grp": 1 - side, "tp": me}
+        )
+
+    def weights_late(half):
+        block = 2 * (2 * (inner + 3 - 2 * inner) + y) + half
+        return pltpu.make_async_remote_copy(
+            wq_hbm.at[block, pl.ds(depth - LATE, LATE)], wq_late.at[half], late_send, late_recv,
+            device_id={"tp": peers[2]},
+        )
+
+    def every(ref, send_sem, recv_sem):
+        return pltpu.make_async_remote_copy(ref, ref, send_sem, recv_sem, device_id={"tp": mate})
+
+    def shared_q(k):
+        return wq.at[k, :, pl.ds(0, depth - k * LATE // 2), pl.ds(0, HD)]
+
+    def weights_arrive(k):
+        for kv in (1, 0):
+            whole = wkv.at[k, :, pl.ds(0, kv_cols)] if kv else wq.at[k, :, :, pl.ds(0, HD)]
+            for sem in (own_sem, wy_recv):
+                every(whole, sem.at[k, kv], sem.at[k, kv]).wait_recv()
+            every(whole if kv else shared_q(k), wx_recv.at[k, kv], wx_recv.at[k, kv]).wait_recv()
 
     for k in range(2):
-        for part in range(4):
-            weights_own(k, part).start()
-
+        for half in range(2):
+            for kv in range(2):
+                weights_own(k, half, kv).start()
+
+    wq[1, :, depth - LATE :, 2 * HD : 3 * HD] = jnp.zeros((2, LATE, HD), jnp.bfloat16)
     loads[0].wait()
     gain = gain_ref[...]
     for r in range(count // 128):
@@ -365,19 +389,27 @@
         top = jnp.max(jnp.abs(weighted), axis=1, keepdims=True)
         stat_own[pl.ds(r, 1), :] = jnp.transpose(jnp.broadcast_to(square, (128, 128)))[0:1, :]
         stat_own[pl.ds(4 + r, 1), :] = jnp.transpose(jnp.broadcast_to(top, (128, 128)))[0:1, :]
-    stats[me] = stat_own[...]
+    loads[-2].wait()
     loads[-1].wait()
 
     pl.semaphore_wait(barrier, n)
 
+    def stat_pair():
+        return pltpu.make_async_remote_copy(
+            stat_own, stat_mate, st_send.at[0], st_recv.at[0], device_id={"tp": mate}
+        )
+
     def stat_copy(d):
         return pltpu.make_async_remote_copy(
-            stat_own, stats.at[me], st_send, st_recv, device_id={"tp": lax.rem(me + d, n)}
+            stats.at[chip], stats.at[chip], st_send.at[1], st_recv.at[1],
+            device_id={"tp": lax.rem(me + 2 * d, n)},
         )
 
     def stat_all():
-        others = stats.at[pl.ds(1, n - 1)]
-        return pltpu.make_async_remote_copy(others, others, st_send, st_recv, device_id={"tp": mate})
+        others = stats.at[pl.ds(1, n // 2 - 1)]
+        return pltpu.make_async_remote_copy(
+            others, others, st_send.at[1], st_recv.at[1], device_id={"tp": mate}
+        )
 
     def act_mate():
         return pltpu.make_async_remote_copy(
@@ -399,16 +431,32 @@
             piece, piece, mate_send, mate_recv.at[p], device_id={"tp": mate}
         )
 
-    forwarded = [(s, part) for part in (2, 3, 0, 1) for s in (2, 3)]
-    lax.fori_loop(1, n, lambda d, c: (stat_copy(d).start(), c)[1], 0)
-    for s, part in forwarded:
-        weights_to(s, side, part).start()
-    for p in everyone:
-        act_across(p).start()
+    forwarded = [(s, k, kv) for k in (0, 1) for kv in (1, 0) for s in (2, 3)]
+    def weights_beside_all(k, kv):
+        for half in range(2):
+            weights_beside(k, half, kv).start()
+
+    stat_pair().start()
+    for each in forwarded[:2]:
+        weights_far(*each).start()
+    weights_beside_all(0, 1)
+    stat_pair().wait()
+    mine, other = stat_own[...], stat_mate[...]
+    stats[chip, 0:4] = mine[0:4] + other[0:4]
+    stats[chip, 4:8] = jnp.maximum(mine[4:8], other[4:8])
+    lax.fori_loop(1, n // 2, lambda d, c: (stat_copy(d).start(), c)[1], 0)
+    for each in forwarded[2:]:
+        weights_far(*each).start()
+
+    @pl.when(is_mid)
+    def _():
+        for p in everyone:
+            act_across(p).start()
+
     act_mate().start()
-    for k in range(2):
-        for part in range(4):
-            weights_to(1, k, part).start()
+    weights_beside_all(0, 0)
+    weights_beside_all(1, 1)
+    weights_beside_all(1, 0)
 
     even = lax.rem(lax.broadcasted_iota(jnp.int32, (128, HD), 1), 2) == 0
     token = lax.broadcasted_iota(jnp.int32, (128, HD), 0) + prefix_ref[0]
@@ -418,6 +466,18 @@
         cosine[pl.ds(r * 128, 128), :] = jnp.cos(angle)
         turn = jnp.sin(angle)
         sine[pl.ds(r * 128, 128), :] = jnp.where(even, -turn, turn)
+
+    for each in forwarded[:-1]:
+        weights_far(*each).wait_recv()
+        weights_twin(*each).start()
+
+    @pl.when(is_end)
+    def _():
+        for p in everyone:
+            act_across(p).start()
+
+    weights_far(*forwarded[-1]).wait_recv()
+    weights_twin(*forwarded[-1]).start()
 
     stat_all().wait()
     everything = stats[...]
@@ -435,10 +495,6 @@
             weighted = h_ref[block, lanes].astype(jnp.float32) * gain_ref[:, lanes]
             payload_out[block, lanes] = (weighted * inv / scale).astype(jnp.bfloat16)
 
-    for s, part in forwarded:
-        weights_to(s, side, part).wait_recv()
-        weights_twin(s, part).start()
-
     @pl.when(is_mid)
     def _():
         for p in everyone:
@@ -446,11 +502,7 @@
             act_pass(p).start()
 
     act_mate().wait_recv()
-    for part in (0, 2):
-        whole = weights_all(own_sem.at[part // 2], own_sem.at[part // 2], part)
-        whole.wait_recv()
-        weights_all(w_send.at[part // 2], w_recv.at[part // 2], part).wait()
-        weights_all(wx_send.at[part // 2], wx_recv.at[part // 2], part).wait()
+    weights_arrive(0)
 
     def product(slot, block, k, half):
         return jnp.dot(gath[slot, block, :], wq[k, half], preferred_element_type=jnp.float32)
@@ -465,11 +517,20 @@
         kvacc[p] = kv_product(0, block, 0, 0) + kv_product(1, block, 0, 1)
         acc[block, :] = product(0, block, 0, 0) + product(1, block, 0, 1)
 
-    def q_partial(s, p):
-        block = pl.ds(p * rows, rows)
-        return pltpu.make_async_remote_copy(
-            q_give.at[s - 1, block], q_got.at[s - 1, block], pq_send, pq_recv.at[p],
-            device_id={"tp": peers[s]},
+    weights_arrive(1)
+
+    def q_beside(p):
+        block = pl.ds(p * rows, rows)
+        return pltpu.make_async_remote_copy(
+            q_give.at[pl.ds(0, 2), block], q_got.at[pl.ds(0, 2), block], pq_send.at[0], pq_recv.at[0, p],
+            device_id={"tp": beside},
+        )
+
+    def q_along(p):
+        block = pl.ds(p * rows, rows)
+        return pltpu.make_async_remote_copy(
+            q_give.at[2, block], q_got.at[2, block], pq_send.at[1], pq_recv.at[1, p],
+            device_id={"tp": peers[2]},
         )
 
     def kv_partial(s, p):
@@ -489,15 +550,28 @@
         pair = kvacc[p] + kv_product(3 - core, block, 1, 1 - core)
         kvacc[p] = pair
         for s in range(1, 4):
-            kv_give[s - 1, p] = pair[s * kv_cols : (s + 1) * kv_cols, :]
+            kv_give[s - 1, p] = pair[s * kv_cols : (s + 1) * kv_cols, :].astype(jnp.bfloat16)
         for s in range(1, 4):
             kv_partial(s, p).start()
         whole = acc[block, :] + product(3 - core, block, 1, 1 - core)
-        acc[block, 0:HD] = whole[:, 0:HD]
-        for s in range(1, 4):
-            q_give[s - 1, block, :] = whole[:, s * HD : (s + 1) * HD].astype(jnp.bfloat16)
-        for s in range(1, 4):
-            q_partial(s, p).start()
+        acc[block, :] = whole
+        q_give[0, block, :] = whole[:, HD : 2 * HD].astype(jnp.bfloat16)
+        q_give[1, block, :] = whole[:, 3 * HD :].astype(jnp.bfloat16)
+        q_beside(p).start()
+
+    def late_arrive():
+        every(wq_late, late_recv, late_recv).wait_recv()
+
+    def q_combine(p):
+        block = pl.ds(p * rows, rows)
+        x = acc[block, 2 * HD : 3 * HD]
+        for half in range(2):
+            x = x + jnp.dot(
+                gath[2 + half, block, depth - LATE :], wq_late[half], preferred_element_type=jnp.float32
+            )
+        q_beside(p).wait_recv()
+        q_give[2, block, :] = (x + q_got[1, block, :].astype(jnp.float32)).astype(jnp.bfloat16)
+        q_along(p).start()
 
     kv_scale = jnp.concatenate([scale_ref[:, HD:], jnp.zeros((1, 128 - kv_cols), jnp.float32)], axis=1)
     kv_scale = spread(kv_scale)[0:kv_cols, :]
@@ -505,21 +579,29 @@
 
     def kv_copy(p, d):
         return pltpu.make_async_remote_copy(
-            kv_own.at[p], kv_all.at[me, p], kv_send, kv_recv.at[p], device_id={"tp": lax.rem(me + d, n)}
-        )
-
-    def every(ref, send_sem, recv_sem):
-        return pltpu.make_async_remote_copy(ref, ref, send_sem, recv_sem, device_id={"tp": mate})
+            kv_own.at[p], kv_tail.at[me] if p == last else kv_all.at[core, chip, p], kv_send.at[int(p == last)], kv_recv.at[p],
+            device_id={"tp": lax.rem(me + d, n)},
+        )
+
+    kv_final = kv_tail.at[pl.ds(1, n - 1)]
+    kv_mine = kv_all.at[core, :, pl.ds(0, last)]
+    kv_spread_all = pltpu.make_async_remote_copy(
+        kv_mine, kv_mine, kv_send.at[2], kv_recv.at[GRID_PIECES], device_id={"tp": mate}
+    )
 
     def kv_reduce(p):
         total = kvacc[p, 0:kv_cols, :]
         every(kv_got.at[:, p], pkv_send, pkv_recv.at[p]).wait_recv()
         for s in range(1, 4):
-            total = total + kv_got[s - 1, p]
+            total = total + kv_got[s - 1, p].astype(jnp.float32)
         mine = (total * inv_row[p : p + 1, :] * kv_scale).astype(jnp.bfloat16)
         kv_own[p] = mine
-        kv_all[me, p] = mine
-        lax.fori_loop(1, n, lambda d, c: (kv_copy(p, d).start(), c)[1], 0)
+        if p == last:
+            kv_tail[me] = mine
+            lax.fori_loop(1, n, lambda d, c: (kv_copy(p, d).start(), c)[1], 0)
+        else:
+            kv_all[core, chip, p] = mine
+            lax.fori_loop(1, n // 2, lambda d, c: (kv_copy(p, 2 * d).start(), c)[1], 0)
 
     def rotated(x, block):
         swapped = jnp.where(even, pltpu.roll(x, HD - 1, 1), pltpu.roll(x, 1, 1))
@@ -528,30 +610,39 @@
     def q_reduce(p):
         block = pl.ds(p * rows, rows)
         x = acc[block, 0:HD]
-        every(q_got.at[:, block], pq_send, pq_recv.at[p]).wait_recv()
-        for s in range(1, 4):
-            x = x + q_got[s - 1, block, :].astype(jnp.float32)
+        q_along(p).wait_recv()
+        x = x + q_got[0, block, :].astype(jnp.float32) + q_got[2, block, :].astype(jnp.float32)
         q_out[block, :] = rotated(x * inv_col[block, :] * qscale, block)
 
     def heads(p):
         block = pl.ds(p * rows, rows)
-        every(kv_all.at[pl.ds(1, n - 1), p], kv_send, kv_recv.at[p]).wait_recv()
-        pair = kv_all[:, p].astype(jnp.float32)
+        if p == last:
+            every(kv_final, kv_send.at[1], kv_recv.at[p]).wait_recv()
+        elif p == 0:
+            kv_spread_all.wait_recv()
+        if p == last:
+            pair = kv_tail[...].astype(jnp.float32)
+        else:
+            both = kv_all[:, :, p].astype(jnp.float32)
+            pair = jnp.stack([both[0], both[1]], axis=1).reshape(n, kv_cols, 128)
         keys = jnp.transpose(pair[:, 0:KV_COLS_DEV, :].reshape(HD, 128))
         k_out[block, :] = rotated(keys, block)
         values = jnp.transpose(pair[:, KV_COLS_DEV:, :].reshape(HD, 128))
         v_out[block, :] = values.astype(jnp.bfloat16)
 
-    last = GRID_PIECES - 1
-
     @pl.when(is_mid)
     def _():
         for p in everyone:
             near(p)
         for p in everyone:
             far(p)
-        for p in range(last):
+        for half in range(2):
+            weights_late(half).start()
+        for p in everyone:
             kv_reduce(p)
+        late_arrive()
+        for p in everyone:
+            q_combine(p)
 
     @pl.when(is_end)
     def _():
@@ -560,23 +651,38 @@
             act_pass(p).start()
             near(p)
             far(p)
-            if p:
-                kv_reduce(p - 1)
-
+            if p == last - 1:
+                for half in range(2):
+                    weights_late(half).start()
+        for p in everyone:
+            kv_reduce(p)
+        late_arrive()
+        for p in everyone:
+            q_combine(p)
+
+    for p in range(last):
+        every(kv_all.at[0, pl.ds(1, n // 2 - 1), p], kv_recv.at[p], kv_recv.at[p]).wait_recv()
+    kv_spread_all.start()
+    for p in range(last):
+        q_reduce(p)
     every(gath.at[0], act_send, act_send).wait_send()
     every(gath.at[pl.ds(0, 2)], mate_send, mate_send).wait_send()
-    for part in (0, 2):
-        weights_all(w_send.at[2 + part // 2], w_send.at[2 + part // 2], part).wait_send()
-
-    for p in range(last):
-        q_reduce(p)
-    kv_reduce(last)
+    for i in (1, 4, 7):
+        every(wkv.at[:, :, pl.ds(0, kv_cols)], w_send.at[i], w_send.at[i]).wait_send()
+    every(wq.at[:, :, :, pl.ds(0, HD)], w_send.at[0], w_send.at[0]).wait_send()
+    for i in (2, 5):
+        for k in range(2):
+            every(shared_q(k), w_send.at[i + k], w_send.at[i + k]).wait_send()
+    every(wq_late, late_send, late_send).wait_send()
     for p in range(last):
         heads(p)
     q_reduce(last)
     every(kv_give, pkv_send, pkv_send).wait_send()
-    every(q_give, pq_send, pq_send).wait_send()
-    every(kv_all.at[pl.ds(1, n - 1)], kv_send, kv_send).wait_send()
+    every(q_give.at[pl.ds(0, 2)], pq_send.at[0], pq_send.at[0]).wait_send()
+    every(q_give.at[2], pq_send.at[1], pq_send.at[1]).wait_send()
+    every(kv_all.at[0, pl.ds(1, n // 2 - 1)], kv_send.at[0], kv_send.at[0]).wait_send()
+    every(kv_final, kv_send.at[1], kv_send.at[1]).wait_send()
+    kv_spread_all.wait_send()
     heads(last)
 
 
@@ -589,16 +695,19 @@
         pltpu.VMEM((4, count, depth), bf16),
         pltpu.VMEM((2, 2, depth, 4 * HD), bf16),
         pltpu.VMEM((2, 2, 4 * kv_cols, depth), bf16),
+        pltpu.VMEM((2, LATE, HD), bf16),
         pltpu.VMEM((count, 4 * HD), f32),
         pltpu.VMEM((pieces, 4 * kv_cols, rows), f32),
         pltpu.VMEM((3, count, HD), bf16),
         pltpu.VMEM((3, count, HD), bf16),
-        pltpu.VMEM((3, pieces, kv_cols, rows), f32),
-        pltpu.VMEM((3, pieces, kv_cols, rows), f32),
+        pltpu.VMEM((3, pieces, kv_cols, rows), bf16),
+        pltpu.VMEM((3, pieces, kv_cols, rows), bf16),
         pltpu.VMEM((8, 128), f32),
-        pltpu.VMEM((16, 8, 128), f32),
+        pltpu.VMEM((8, 128), f32),
+        pltpu.VMEM((8, 8, 128), f32),
         pltpu.VMEM((pieces, kv_cols, rows), bf16),
-        pltpu.VMEM((16, pieces, kv_cols, rows), bf16),
+        pltpu.VMEM((2, 8, pieces - 1, kv_cols, rows), bf16),
+        pltpu.VMEM((16, kv_cols, rows), bf16),
         pltpu.VMEM((count // 128, 128), f32),
         pltpu.VMEM((count, HD), f32),
         pltpu.VMEM((count, HD), f32),
@@ -606,24 +715,27 @@
         pltpu.VMEM((count, depth), bf16),
         pltpu.VMEM((1, depth), f32),
         pltpu.VMEM((1, HD + kv_cols), f32),
-        dma((count // 128 + 2,)),
-        dma((2,)),
+        pltpu.VMEM((1, HD), f32),
+        dma((count // 128 + 3,)),
+        dma((2, 2)),
         dma,
         dma,
-        dma((4,)),
-        dma((10,)),
         dma((2,)),
         dma((2,)),
+        dma((8,)),
+        dma((2, 2, 2)),
+        dma((2, 2)),
+        dma((2, 2)),
         dma,
         dma((pieces,)),
         dma,
         dma((pieces + 1,)),
+        dma((2,)),
+        dma((2, pieces)),
         dma,
         dma((pieces,)),
-        dma,
-        dma((pieces,)),
-        dma,
-        dma((pieces,)),
+        dma((3,)),
+        dma((pieces + 1,)),
     ]
 
 
@@ -668,7 +780,7 @@
             pltpu.VMEM((count // 128, 128), f32),
         ),
         in_specs=[pl.BlockSpec(memory_space=pltpu.SMEM)]
-        + ([hbm, hbm, vmem] + [hbm] * 3 if grid else [vmem] * 5 + [hbm] * 2),
+        + ([hbm] * 6 if grid else [vmem] * 5 + [hbm] * 2),
         out_specs=(vmem,) * 5,
         scratch_shapes=grid_scratch(count, depth) if grid else [
             pltpu.VMEM((chips, count, depth), bf16),

time: 73.3 us -> 69.3 us (0.945)
  Pallas kernels: 71.8 us -> 67.9 us
    pallas_call x1, Pallas kernels: 70.7 us -> 66.7 us  [local(): pl.pallas_call(functools.partial(grid_kernel, width) if grid else functoo...]
where the time goes in v3:
time: 69.3 us; the launch traced here: 69.1 us
  Pallas kernels  67.9 us (98%)
  between operations  1.29 us (2%)
    pallas_call x1, Pallas kernels, local(): pl.pallas_call(functools.partial(grid_kernel, width) if grid else functoo...  66.7 us

profile of v3, /device:TPU:0, one launch (start us, length us, event | category | flops | bytes accessed | tf_op | source)
XLA Modules:
  0.0 69.1 jit_solution(7804398144641888140)
XLA Ops:
  1.3 66.7 %shard_map.110 = (bf16[512,128]{1,0:T(8,128)(2,1)S(1)}, bf16[512,128]{1,0:T(8,128)(2,1)S(1)}, bf16[512,128]{1,0:T(8,128)(2,1)S(1)}, bf16[512,1024]{1,0:T(8,128)(2,1)S(1)}, f32[4,128]{1,0:T(4,128)S(1)}) custom-call(s32[1]{0:T(128)S(6)} %copy.12.prefix_ref, bf16[512,1024]{1,0:T(8,128)(2,1)} %h_hbm.1, f32[1,1024]{1,0:T(1,128)} %bitcast.5, ...), custom_call_target="tpu_custom_call" | custom-call | tf_op jit(solution)/shard_map/pallas_call | solution.py:773
  68.0 1.1 %shard_map.111 = (bf16[512,128]{1,0:T(8,128)(2,1)}, bf16[512,128]{1,0:T(8,128)(2,1)}, bf16[512,128]{1,0:T(8,128)(2,1)}, bf16[512,1024]{1,0:T(8,128)(2,1)}, f32[4,128]{1,0:T(4,128)}) custom-call(bf16[512,128]{1,0:T(8,128)(2,1)S(1)} %get-tuple-element.15.refs_0_, bf16[512,128]{1,0:T(8,128)(2,1)S(1)} %get-tuple-element.16.refs_1_, ...), custom_call_target="tpu_custom_call" | custom-call | tf_op jit(solution)/shard_map/pallas_call | solution.py:752

commit v4 on v3

--- a/solution.py
+++ b/solution.py
@@ -15,7 +15,7 @@
 rope_base = 500000.0
 PIECES = 2
 GRID_PIECES = 4
-LATE = 384
+LATE = 256
 
 
 def ring_order(chips):
@@ -277,7 +277,7 @@
     q_out, k_out, v_out, payload_out, rs_out,
     gath, wq, wkv, wq_late, acc, kvacc, q_give, q_got, kv_give, kv_got,
     stat_own, stat_mate, stats, kv_own, kv_all, kv_tail, inv_row, inv_col, cosine, sine,
-    h_ref, gain_ref, scale_ref, freq_ref, in_sem, own_sem, late_send, late_recv,
+    h_ref, gain_ref, scale_ref, freq_ref, in_sem, own_sem, late_send, late_recv, met,
     st_send, st_recv, w_send, w_recv, wx_recv, wy_recv, act_send, act_recv, mate_send, mate_recv,
     pq_send, pq_recv, pkv_send, pkv_recv, kv_send, kv_recv,
 ):
@@ -304,12 +304,13 @@
 
     barrier = pltpu.get_barrier_semaphore()
 
-    def greet(d, carry):
-        pl.semaphore_signal(barrier, inc=1, device_id={"tp": lax.rem(me + d, n)})
-        return carry
-
-    lax.fori_loop(1, n, greet, 0)
+    for peer in [mate] + peers[1:]:
+        pl.semaphore_signal(barrier, inc=1, device_id={"tp": peer})
     pl.semaphore_signal(barrier, inc=1, device_id={"grp": 1 - side, "tp": me})
+
+    @pl.when(is_mid)
+    def _():
+        pl.semaphore_signal(barrier, inc=1, device_id={"tp": across})
 
     loads = [pltpu.make_async_copy(gain_hbm, gain_ref, in_sem.at[0])]
     for r in range(count // 128):
@@ -392,7 +393,13 @@
     loads[-2].wait()
     loads[-1].wait()
 
-    pl.semaphore_wait(barrier, n)
+    @pl.when(is_mid)
+    def _():
+        pl.semaphore_wait(barrier, 6)
+
+    @pl.when(is_end)
+    def _():
+        pl.semaphore_wait(barrier, 5)
 
     def stat_pair():
         return pltpu.make_async_remote_copy(
@@ -437,21 +444,41 @@
             weights_beside(k, half, kv).start()
 
     stat_pair().start()
-    for each in forwarded[:2]:
+    for each in forwarded[:4]:
         weights_far(*each).start()
     weights_beside_all(0, 1)
+
+    @pl.when(is_mid)
+    def _():
+        for p in everyone:
+            act_across(p).start()
+        pl.semaphore_signal(met.at[1], inc=1, device_id={"tp": across})
+
+    pl.semaphore_signal(met.at[0], inc=1, device_id={"tp": mate})
+    pl.semaphore_wait(met.at[0], 1)
+
+    @pl.when(is_mid)
+    def _():
+        pl.semaphore_wait(met.at[1], 1)
+
+    pl.semaphore_signal(met.at[2], inc=1, device_id={"tp": mate})
+    pl.semaphore_wait(met.at[2], 1)
+
+    @pl.when(is_mid)
+    def _():
+        pl.semaphore_signal(met.at[3], inc=1, device_id={"tp": peers[2]})
+
+    @pl.when(is_end)
+    def _():
+        pl.semaphore_wait(met.at[3], 1)
+
     stat_pair().wait()
     mine, other = stat_own[...], stat_mate[...]
     stats[chip, 0:4] = mine[0:4] + other[0:4]
     stats[chip, 4:8] = jnp.maximum(mine[4:8], other[4:8])
     lax.fori_loop(1, n // 2, lambda d, c: (stat_copy(d).start(), c)[1], 0)
-    for each in forwarded[2:]:
+    for each in forwarded[4:]:
         weights_far(*each).start()
-
-    @pl.when(is_mid)
-    def _():
-        for p in everyone:
-            act_across(p).start()
 
     act_mate().start()
     weights_beside_all(0, 0)
@@ -467,7 +494,7 @@
         turn = jnp.sin(angle)
         sine[pl.ds(r * 128, 128), :] = jnp.where(even, -turn, turn)
 
-    for each in forwarded[:-1]:
+    for each in forwarded:
         weights_far(*each).wait_recv()
         weights_twin(*each).start()
 
@@ -476,8 +503,6 @@
         for p in everyone:
             act_across(p).start()
 
-    weights_far(*forwarded[-1]).wait_recv()
-    weights_twin(*forwarded[-1]).start()
 
     stat_all().wait()
     everything = stats[...]
@@ -638,11 +663,12 @@
             far(p)
         for half in range(2):
             weights_late(half).start()
-        for p in everyone:
+        for p in range(last):
             kv_reduce(p)
         late_arrive()
         for p in everyone:
             q_combine(p)
+        kv_reduce(last)
 
     @pl.when(is_end)
     def _():
@@ -720,6 +746,7 @@
         dma((2, 2)),
         dma,
         dma,
+        pltpu.SemaphoreType.REGULAR((4,)),
         dma((2,)),
         dma((2,)),
         dma((8,)),

time: 69.3 us -> 68.8 us (level)
  no operation moved by 1% of the time
where the time goes in v4:
time: 68.8 us; the launch traced here: 68.6 us
  Pallas kernels  67.3 us (98%)
  between operations  1.29 us (2%)
    pallas_call x1, Pallas kernels, local(): pl.pallas_call(functools.partial(grid_kernel, width) if grid else functoo...  66.2 us

profile of v4, /device:TPU:0, one launch (start us, length us, event | category | flops | bytes accessed | tf_op | source)
XLA Modules:
  0.0 68.6 jit_solution(13655455706293089869)
XLA Ops:
  1.3 66.2 %shard_map.110 = (bf16[512,128]{1,0:T(8,128)(2,1)S(1)}, bf16[512,128]{1,0:T(8,128)(2,1)S(1)}, bf16[512,128]{1,0:T(8,128)(2,1)S(1)}, bf16[512,1024]{1,0:T(8,128)(2,1)S(1)}, f32[4,128]{1,0:T(4,128)S(1)}) custom-call(s32[1]{0:T(128)S(6)} %copy.12.prefix_ref, bf16[512,1024]{1,0:T(8,128)(2,1)} %h_hbm.1, f32[1,1024]{1,0:T(1,128)} %bitcast.5, ...), custom_call_target="tpu_custom_call" | custom-call | tf_op jit(solution)/shard_map/pallas_call | solution.py:800
  67.5 1.1 %shard_map.111 = (bf16[512,128]{1,0:T(8,128)(2,1)}, bf16[512,128]{1,0:T(8,128)(2,1)}, bf16[512,128]{1,0:T(8,128)(2,1)}, bf16[512,1024]{1,0:T(8,128)(2,1)}, f32[4,128]{1,0:T(4,128)}) custom-call(bf16[512,128]{1,0:T(8,128)(2,1)S(1)} %get-tuple-element.15.refs_0_, bf16[512,128]{1,0:T(8,128)(2,1)S(1)} %get-tuple-element.16.refs_1_, ...), custom_call_target="tpu_custom_call" | custom-call | tf_op jit(solution)/shard_map/pallas_call | solution.py:779

commit v5 on v4

--- a/solution.py
+++ b/solution.py
@@ -304,7 +304,7 @@
 
     barrier = pltpu.get_barrier_semaphore()
 
-    for peer in [mate] + peers[1:]:
+    for peer in [mate] + peers[1:3]:
         pl.semaphore_signal(barrier, inc=1, device_id={"tp": peer})
     pl.semaphore_signal(barrier, inc=1, device_id={"grp": 1 - side, "tp": me})
 
@@ -378,6 +378,26 @@
                 weights_own(k, half, kv).start()
 
     wq[1, :, depth - LATE :, 2 * HD : 3 * HD] = jnp.zeros((2, LATE, HD), jnp.bfloat16)
+    @pl.when(is_mid)
+    def _():
+        pl.semaphore_wait(barrier, 5)
+
+    @pl.when(is_end)
+    def _():
+        pl.semaphore_wait(barrier, 4)
+
+    forwarded = [(2, 0, 1), (2, 0, 0), (3, 0, 1), (3, 0, 0), (2, 1, 1), (3, 1, 1), (2, 1, 0), (3, 1, 0)]
+
+    def weights_beside_all(k, kv):
+        for half in range(2):
+            weights_beside(k, half, kv).start()
+
+    for each in forwarded[:2]:
+        weights_far(*each).start()
+    weights_beside_all(0, 1)
+    pl.semaphore_signal(met.at[0], inc=1, device_id={"tp": mate})
+    pl.semaphore_signal(met.at[4], inc=1, device_id={"tp": beside})
+
     loads[0].wait()
     gain = gain_ref[...]
     for r in range(count // 128):
@@ -393,14 +413,6 @@
     loads[-2].wait()
     loads[-1].wait()
 
-    @pl.when(is_mid)
-    def _():
-        pl.semaphore_wait(barrier, 6)
-
-    @pl.when(is_end)
-    def _():
-        pl.semaphore_wait(barrier, 5)
-
     def stat_pair():
         return pltpu.make_async_remote_copy(
             stat_own, stat_mate, st_send.at[0], st_recv.at[0], device_id={"tp": mate}
@@ -438,23 +450,17 @@
             piece, piece, mate_send, mate_recv.at[p], device_id={"tp": mate}
         )
 
-    forwarded = [(s, k, kv) for k in (0, 1) for kv in (1, 0) for s in (2, 3)]
-    def weights_beside_all(k, kv):
-        for half in range(2):
-            weights_beside(k, half, kv).start()
-
     stat_pair().start()
-    for each in forwarded[:4]:
+    pl.semaphore_wait(met.at[4], 1)
+    for each in forwarded[2:4]:
         weights_far(*each).start()
-    weights_beside_all(0, 1)
 
     @pl.when(is_mid)
     def _():
+        pl.semaphore_signal(met.at[1], inc=1, device_id={"tp": across})
         for p in everyone:
             act_across(p).start()
-        pl.semaphore_signal(met.at[1], inc=1, device_id={"tp": across})
-
-    pl.semaphore_signal(met.at[0], inc=1, device_id={"tp": mate})
+
     pl.semaphore_wait(met.at[0], 1)
 
     @pl.when(is_mid)
@@ -746,7 +752,7 @@
         dma((2, 2)),
         dma,
         dma,
-        pltpu.SemaphoreType.REGULAR((4,)),
+        pltpu.SemaphoreType.REGULAR((5,)),
         dma((2,)),
         dma((2,)),
         dma((8,)),

time: 68.8 us -> 67.8 us (0.985)
  Pallas kernels: 67.3 us -> 66.4 us
    pallas_call x1, Pallas kernels: 66.2 us -> 65.2 us  [local(): pl.pallas_call(functools.partial(grid_kernel, width) if grid else functoo...]
where the time goes in v5:
time: 67.8 us; the launch traced here: 67.6 us
  Pallas kernels  66.4 us (98%)
  between operations  1.29 us (2%)
    pallas_call x1, Pallas kernels, local(): pl.pallas_call(functools.partial(grid_kernel, width) if grid else functoo...  65.2 us

profile of v5, /device:TPU:0, one launch (start us, length us, event | category | flops | bytes accessed | tf_op | source)
XLA Modules:
  0.0 67.6 jit_solution(17058620448507931460)
XLA Ops:
  1.3 65.2 %shard_map.110 = (bf16[512,128]{1,0:T(8,128)(2,1)S(1)}, bf16[512,128]{1,0:T(8,128)(2,1)S(1)}, bf16[512,128]{1,0:T(8,128)(2,1)S(1)}, bf16[512,1024]{1,0:T(8,128)(2,1)S(1)}, f32[4,128]{1,0:T(4,128)S(1)}) custom-call(s32[1]{0:T(128)S(6)} %copy.12.prefix_ref, bf16[512,1024]{1,0:T(8,128)(2,1)} %h_hbm.1, f32[1,1024]{1,0:T(1,128)} %bitcast.5, ...), custom_call_target="tpu_custom_call" | custom-call | tf_op jit(solution)/shard_map/pallas_call | solution.py:806
  66.5 1.1 %shard_map.111 = (bf16[512,128]{1,0:T(8,128)(2,1)}, bf16[512,128]{1,0:T(8,128)(2,1)}, bf16[512,128]{1,0:T(8,128)(2,1)}, bf16[512,1024]{1,0:T(8,128)(2,1)}, f32[4,128]{1,0:T(4,128)}) custom-call(bf16[512,128]{1,0:T(8,128)(2,1)S(1)} %get-tuple-element.15.refs_0_, bf16[512,128]{1,0:T(8,128)(2,1)S(1)} %get-tuple-element.16.refs_1_, ...), custom_call_target="tpu_custom_call" | custom-call | tf_op jit(solution)/shard_map/pallas_call | solution.py:785

commit v6 on v5

--- a/solution.py
+++ b/solution.py
@@ -15,7 +15,7 @@
 rope_base = 500000.0
 PIECES = 2
 GRID_PIECES = 4
-LATE = 256
+LATE = 128
 
 
 def ring_order(chips):

time: 67.8 us -> 67.5 us (level)
  no operation moved by 1% of the time
where the time goes in v6:
time: 67.5 us; the launch traced here: 67.3 us
  Pallas kernels  66 us (98%)
  between operations  1.29 us (2%)
    pallas_call x1, Pallas kernels, local(): pl.pallas_call(functools.partial(grid_kernel, width) if grid else functoo...  64.9 us

profile of v6, /device:TPU:0, one launch (start us, length us, event | category | flops | bytes accessed | tf_op | source)
XLA Modules:
  0.0 67.3 jit_solution(11212854978246039985)
XLA Ops:
  1.3 64.9 %shard_map.110 = (bf16[512,128]{1,0:T(8,128)(2,1)S(1)}, bf16[512,128]{1,0:T(8,128)(2,1)S(1)}, bf16[512,128]{1,0:T(8,128)(2,1)S(1)}, bf16[512,1024]{1,0:T(8,128)(2,1)S(1)}, f32[4,128]{1,0:T(4,128)S(1)}) custom-call(s32[1]{0:T(128)S(6)} %copy.12.prefix_ref, bf16[512,1024]{1,0:T(8,128)(2,1)} %h_hbm.1, f32[1,1024]{1,0:T(1,128)} %bitcast.5, ...), custom_call_target="tpu_custom_call" | custom-call | tf_op jit(solution)/shard_map/pallas_call | solution.py:806
  66.2 1.1 %shard_map.111 = (bf16[512,128]{1,0:T(8,128)(2,1)}, bf16[512,128]{1,0:T(8,128)(2,1)}, bf16[512,128]{1,0:T(8,128)(2,1)}, bf16[512,1024]{1,0:T(8,128)(2,1)}, f32[4,128]{1,0:T(4,128)}) custom-call(bf16[512,128]{1,0:T(8,128)(2,1)S(1)} %get-tuple-element.15.refs_0_, bf16[512,128]{1,0:T(8,128)(2,1)S(1)} %get-tuple-element.16.refs_1_, ...), custom_call_target="tpu_custom_call" | custom-call | tf_op jit(solution)/shard_map/pallas_call | solution.py:785
